TPU v7x, 32 devices: a 4x2x2 block of a 4x4x8 slice. The times are simulated.
32 devices in a mesh: dp: 4 (over y, z), sp: 8 (over x, core).
Axes of the slice: x: 4, y: 2, z: 2, core: 2. Of those that a mesh axis runs over, the one named last changes fastest.
The devices are a block of a 4x4x8 slice.
Arguments:
- signal: bfloat16 [262144, 256], P(('dp', 'sp')), parts along dimension 0
- w_first: bfloat16 [11, 2048, 2, 32, 32], P(None, 'sp')
- w_second: bfloat16 [11, 2048, 2, 32, 32], P(None, 'sp')
Outputs:
- output: bfloat16 [262144, 256], P(('dp', 'sp')), parts along dimension 0
There are 4 independent parts. A program takes and returns all parts, laid end to end along the dimension named above; an argument that names none is the same for every part.
All inputs are finite; a program needn't handle non-finite values.
Results may differ from a plain program's by a relative error of at most 0.02.
Values are sent between devices in bfloat16 or wider.
A program may use at most 768 MiB of HBM per device.

v0:
```python
import jax
import jax.numpy as jnp
from jax import lax
from jax.sharding import PartitionSpec as P


def local_partner(act_blocks, distance):
    num_blocks = act_blocks.shape[0]
    grouped = act_blocks.reshape(num_blocks // (2 * distance), 2, distance, act_blocks.shape[1], act_blocks.shape[2])
    return grouped[:, ::-1].reshape(act_blocks.shape)


def mix_blocks(act_blocks, partner, weights):
    own_part = jnp.einsum("lij,ljc->lic", weights[:, 0], act_blocks, preferred_element_type=jnp.float32)
    cross_part = jnp.einsum("lij,ljc->lic", weights[:, 1], partner, preferred_element_type=jnp.float32)
    return (own_part + cross_part).astype(jnp.bfloat16)


def solution(mesh):
    groups = mesh.shape["sp"]

    def apply_map(act_blocks, weights, distances):
        local_blocks = act_blocks.shape[0]
        for stage, distance in enumerate(distances):
            if distance < local_blocks:
                partner = local_partner(act_blocks, distance)
            else:
                dev_step = distance // local_blocks
                pairing = [(device, device ^ dev_step) for device in range(groups)]
                partner = lax.ppermute(act_blocks, "sp", pairing)
            act_blocks = mix_blocks(act_blocks, partner, weights[stage])
        return act_blocks

    def device_program(signal, w_first, w_second):
        stages = w_first.shape[0]
        local_blocks = w_first.shape[1]
        block_rows = w_first.shape[3]
        act_blocks = signal.reshape(local_blocks, block_rows, signal.shape[1])
        dist_down = [2 ** (stages - 1 - level) for level in range(stages)]
        hidden = apply_map(act_blocks, w_first, dist_down)
        hidden = jax.nn.gelu(hidden.astype(jnp.float32), approximate=False).astype(jnp.bfloat16)
        result = apply_map(hidden, w_second, dist_down[::-1])
        return result.reshape(signal.shape)

    row_spec = P(("dp", "sp"), None)
    weight_spec = P(None, "sp", None, None, None)
    return jax.shard_map(device_program, mesh=mesh, in_specs=(row_spec, weight_spec, weight_spec), out_specs=row_spec, check_vma=False)
```

profile of v0, /device:TPU:81, one launch (start us, length us, event | category | flops | bytes accessed | tf_op | source)
XLA Modules:
  0.0 820.5 jit_solution(1366791050605131521)
XLA Ops:
  3.8 8.1 fusion.56
  11.9 7.2 copy.47
  23.3 70.1 %collective-permute-done = bf16[256,32,256]{2,1,0:T(8,128)(2,1)} collective-permute-done((bf16[256,32,256]{2,1,0:T(8,128)(2,1)}, bf16[256,32,256]{2,1,0:T(8,128)(2,1)}, u32[]{:S(2)}, u32[]{:S(2)}) %collective-permute-start) | collective-permute-done | bytes 4194336 | tf_op jit(solution)/shard_map/ppermute | solution.py:30
  93.5 5.6 add_convert_fusion.21
  100.9 7.3 copy.46
  112.4 77.6 %collective-permute-done.1 = bf16[256,32,256]{2,1,0:T(8,128)(2,1)} collective-permute-done((bf16[256,32,256]{2,1,0:T(8,128)(2,1)}, bf16[256,32,256]{2,1,0:T(8,128)(2,1)}, u32[]{:S(2)}, u32[]{:S(2)}) %collective-permute-start.1) | collective-permute-done | bytes 4194336 | tf_op jit(solution)/shard_map/ppermute | solution.py:30
  189.9 5.6 add_convert_fusion.20
  198.0 7.3 copy.45
  205.3 7.3 copy.44
  212.6 7.2 copy.43
  219.8 7.6 copy.42
  227.4 7.2 copy.41
  234.6 7.2 copy.40
  241.8 6.4 copy.39
  248.3 6.5 copy.38
  254.7 6.4 copy.37
  261.2 8.0 fusion.55
  269.2 7.2 copy.36
  276.4 7.2 copy.35
  283.6 7.4 copy.34
  291.0 7.3 copy.33
  298.3 7.3 copy.32
  305.5 6.4 copy.31
  312.0 6.4 copy.30
  318.4 6.7 copy.29
  333.1 4.7 fusion.36
  337.8 4.7 rev.48
  342.5 6.6 add_convert_fusion.18
  358.4 6.7 add_convert_fusion.17
  374.4 6.6 add_convert_fusion.16
  381.0 5.0 fusion.39
  386.0 4.8 rev.51
  390.8 6.6 add_convert_fusion.15
  402.1 4.9 rev.52
  407.0 6.6 add_convert_fusion.14
  418.3 5.0 rev.53
  423.3 6.6 add_convert_fusion.13
  430.0 4.7 fusion.42
  434.6 5.1 rev.54
  439.7 6.6 add_convert_fusion.12
  451.0 4.8 rev.55
  455.8 20.9 %fusion.2 = bf16[256,32,256]{2,1,0:T(8,128)(2,1)S(1)} fusion(f32[256,256,32]{1,2,0:T(8,128)} %fusion.43, bf16[256,32,256]{2,1,0:T(8,128)(2,1)} %bitcast.439, bf16[256,2,32,32]{3,2,0,1:T(8,128)(2,1)} %bitcast.435), kind=kOutput, calls=%fused_computation.5 | convolution fusion | flops 276824064 | bytes 18874368 | tf_op jit(solution)/shard_map/lij,ljc->lic/dot_general | solution.py:15
  481.5 4.7 rev.56
  486.2 6.6 add_convert_fusion.10
  497.5 5.1 rev.57
  502.6 6.6 add_convert_fusion.9
  513.9 5.1 rev.58
  518.9 6.6 add_convert_fusion.8
  530.2 4.9 rev.59
  535.1 6.6 add_convert_fusion.7
  541.8 5.0 fusion.48
  546.7 4.8 rev.60
  551.6 6.6 add_convert_fusion.6
  567.5 6.6 add_convert_fusion.5
  583.4 6.6 add_convert_fusion.4
  599.3 8.6 %add_convert_fusion.3 = bf16[256,256,32]{1,2,0:T(8,128)(2,1)} fusion(f32[256,256,32]{1,2,0:T(8,128)} %fusion.51, bf16[256,32,256]{2,1,0:T(8,128)(2,1)} %bitcast.434, bf16[256,2,32,32]{3,2,0,1:T(8,128)(2,1)} %bitcast.377), kind=kOutput, calls=%fused_computation.39 | convolution fusion | flops 138412032 | bytes 18874368 | tf_op jit(solution)/shard_map/lij,ljc->lic/dot_general | solution.py:15
  607.9 6.7 copy.28
  618.8 5.7 add_convert_fusion.2
  626.0 6.5 copy.27
  636.7 79.5 %collective-permute-done.4 = bf16[256,32,256]{2,1,0:T(8,128)(2,1)} collective-permute-done((bf16[256,32,256]{2,1,0:T(8,128)(2,1)}, bf16[256,32,256]{2,1,0:T(8,128)(2,1)}, u32[]{:S(2)}, u32[]{:S(2)}) %collective-permute-start.4) | collective-permute-done | bytes 4194336 | tf_op jit(solution)/shard_map/ppermute | solution.py:30
  716.2 5.6 add_convert_fusion.1
  725.0 6.5 copy.26
  735.7 79.0 %collective-permute-done.5 = bf16[256,32,256]{2,1,0:T(8,128)(2,1)} collective-permute-done((bf16[256,32,256]{2,1,0:T(8,128)(2,1)}, bf16[256,32,256]{2,1,0:T(8,128)(2,1)}, u32[]{:S(2)}, u32[]{:S(2)}) %collective-permute-start.5) | collective-permute-done | bytes 4194336 | tf_op jit(solution)/shard_map/ppermute | solution.py:30
  814.7 5.6 add_convert_fusion
  (114 shorter events, 120.8 us)
Async XLA Ops:
  0.0 93.5 %collective-permute-start = (bf16[256,32,256]{2,1,0:T(8,128)(2,1)}, bf16[256,32,256]{2,1,0:T(8,128)(2,1)}, u32[]{:S(2)}, u32[]{:S(2)}) collective-permute-start(bf16[256,32,256]{2,1,0:T(8,128)(2,1)} %bitcast.437), channel_id=1, source_target_pairs={{0,4},{1,5},{2,6},{3,7},{4,0},{5,1},{6,2},{7,3},{8,12},{9,13},{10,... | collective-permute-start | bytes 12582920 | tf_op jit(solution)/shard_map/ppermute | solution.py:30
  19.1 74.3 %copy-start.35 = (bf16[1,256,2,32,32]{4,3,1,2,0:T(8,128)(2,1)S(1)}, bf16[1,256,2,32,32]{4,3,1,2,0:T(8,128)(2,1)}, u32[]{:S(2)}) copy-start(bf16[1,256,2,32,32]{4,3,1,2,0:T(8,128)(2,1)} %copy.47) | copy-start | bytes 3145732
  99.1 90.9 %collective-permute-start.1 = (bf16[256,32,256]{2,1,0:T(8,128)(2,1)}, bf16[256,32,256]{2,1,0:T(8,128)(2,1)}, u32[]{:S(2)}, u32[]{:S(2)}) collective-permute-start(bf16[256,32,256]{2,1,0:T(8,128)(2,1)} %add_convert_fusion.21), channel_id=1, source_target_pairs={{0,2},{1,3},{2,0},{3,1},{4,6},{5,7},{6,4},{7,5},{8,10},{9,11},{10,... | collective-permute-start | bytes 12582920 | tf_op jit(solution)/shard_map/ppermute | solution.py:30
  108.2 81.8 %copy-start.31 = (bf16[1,256,2,32,32]{4,3,1,2,0:T(8,128)(2,1)S(1)}, bf16[1,256,2,32,32]{4,3,1,2,0:T(8,128)(2,1)}, u32[]{:S(2)}) copy-start(bf16[1,256,2,32,32]{4,3,1,2,0:T(8,128)(2,1)} %copy.46) | copy-start | bytes 3145732
  195.5 133.8 %collective-permute-start.2 = (bf16[256,32,256]{2,1,0:T(8,128)(2,1)}, bf16[256,32,256]{2,1,0:T(8,128)(2,1)}, u32[]{:S(2)}, u32[]{:S(2)}) collective-permute-start(bf16[256,32,256]{2,1,0:T(8,128)(2,1)} %bitcast.9), channel_id=1, source_target_pairs={{0,1},{1,0},{2,3},{3,2},{4,5},{5,4},{6,7},{7,6},{8,9},{9,8},{10,11... | collective-permute-start | bytes 12582920 | tf_op jit(solution)/shard_map/ppermute | solution.py:30
  325.1 4.3 copy-start.30
  329.4 3.8 copy-start.29
  333.1 4.7 copy-start
  342.5 6.6 copy-start.28
  349.1 4.7 copy-start.1
  358.4 6.7 copy-start.27
  365.1 4.7 copy-start.2
  374.4 6.6 copy-start.26
  381.0 5.0 copy-start.3
  390.8 6.7 copy-start.25
  397.4 4.7 copy-start.4
  407.0 6.6 copy-start.24
  413.6 4.7 copy-start.5
  423.3 6.6 copy-start.22
  429.9 4.7 copy-start.6
  439.7 6.6 copy-start.37
  446.3 4.7 copy-start.7
  455.8 21.0 %copy-start.23 = (bf16[1,256,2,32,32]{4,3,1,2,0:T(8,128)(2,1)S(1)}, bf16[1,256,2,32,32]{4,3,1,2,0:T(8,128)(2,1)}, u32[]{:S(2)}) copy-start(bf16[1,256,2,32,32]{4,3,1,2,0:T(8,128)(2,1)} %copy.36) | copy-start | bytes 3145732
  476.8 4.7 copy-start.36
  486.2 6.6 copy-start.21
  492.8 4.7 copy-start.8
  502.6 6.6 copy-start.20
  509.2 4.7 copy-start.9
  518.9 6.6 copy-start.19
  525.6 4.7 copy-start.10
  535.1 6.6 copy-start.18
  541.7 5.0 copy-start.11
  551.6 6.6 copy-start.17
  558.2 4.7 copy-start.12
  567.5 6.6 copy-start.16
  574.2 4.7 copy-start.13
  583.4 6.6 copy-start.15
  590.1 4.7 copy-start.14
  599.3 8.6 %copy-start.40 = (bf16[1,256,2,32,32]{1,4,3,2,0:T(8,128)(2,1)S(1)}, bf16[1,256,2,32,32]{1,4,3,2,0:T(8,128)(2,1)}, u32[]{:S(2)}) copy-start(bf16[1,256,2,32,32]{1,4,3,2,0:T(8,128)(2,1)} %get-tuple-element.13) | copy-start | bytes 3145732
  607.9 10.9 %collective-permute-start.3 = (bf16[256,32,256]{2,1,0:T(8,128)(2,1)}, bf16[256,32,256]{2,1,0:T(8,128)(2,1)}, u32[]{:S(2)}, u32[]{:S(2)}) collective-permute-start(bf16[256,32,256]{2,1,0:T(8,128)(2,1)} %bitcast.110), channel_id=1, source_target_pairs={{0,1},{1,0},{2,3},{3,2},{4,5},{5,4},{6,7},{7,6},{8,9},{9,8},{10,11... | collective-permute-start | bytes 12582920 | tf_op jit(solution)/shard_map/ppermute | solution.py:30
  614.6 4.2 copy-start.32
  618.8 7.2 copy-start.39
  624.5 91.7 %collective-permute-start.4 = (bf16[256,32,256]{2,1,0:T(8,128)(2,1)}, bf16[256,32,256]{2,1,0:T(8,128)(2,1)}, u32[]{:S(2)}, u32[]{:S(2)}) collective-permute-start(bf16[256,32,256]{2,1,0:T(8,128)(2,1)} %bitcast.114), channel_id=1, source_target_pairs={{0,2},{1,3},{2,0},{3,1},{4,6},{5,7},{6,4},{7,5},{8,10},{9,11},{10,... | collective-permute-start | bytes 12582920 | tf_op jit(solution)/shard_map/ppermute | solution.py:30
  632.5 83.8 %copy-start.33 = (bf16[1,256,2,32,32]{4,3,1,2,0:T(8,128)(2,1)S(1)}, bf16[1,256,2,32,32]{4,3,1,2,0:T(8,128)(2,1)}, u32[]{:S(2)}) copy-start(bf16[1,256,2,32,32]{4,3,1,2,0:T(8,128)(2,1)} %copy.27) | copy-start | bytes 3145732
  636.7 88.3 %copy-start.38 = (bf16[1,256,2,32,32]{1,4,3,2,0:T(8,128)(2,1)S(1)}, bf16[1,256,2,32,32]{1,4,3,2,0:T(8,128)(2,1)}, u32[]{:S(2)}) copy-start(bf16[1,256,2,32,32]{1,4,3,2,0:T(8,128)(2,1)} %get-tuple-element.5) | copy-start | bytes 3145732
  721.8 92.9 %collective-permute-start.5 = (bf16[256,32,256]{2,1,0:T(8,128)(2,1)}, bf16[256,32,256]{2,1,0:T(8,128)(2,1)}, u32[]{:S(2)}, u32[]{:S(2)}) collective-permute-start(bf16[256,32,256]{2,1,0:T(8,128)(2,1)} %bitcast.118), channel_id=1, source_target_pairs={{0,4},{1,5},{2,6},{3,7},{4,0},{5,1},{6,2},{7,3},{8,12},{9,13},{10,... | collective-permute-start | bytes 12582920 | tf_op jit(solution)/shard_map/ppermute | solution.py:30
  731.5 83.2 %copy-start.34 = (bf16[1,256,2,32,32]{4,3,1,2,0:T(8,128)(2,1)S(1)}, bf16[1,256,2,32,32]{4,3,1,2,0:T(8,128)(2,1)}, u32[]{:S(2)}) copy-start(bf16[1,256,2,32,32]{4,3,1,2,0:T(8,128)(2,1)} %copy.26) | copy-start | bytes 3145732
where the time goes:
time: 831 us; the launch traced here: 821 us
  waiting for transfers between devices  306 us (37%)
  matrix products  254 us (31%)
  local copies, waits for them, and re-layouts  246 us (30%)
  starting transfers between devices  12.8 us (2%)
    ppermute x6, waiting for transfers between devices, apply_map(): partner = lax.ppermute(act_blocks, 'sp', pairing)  306 us
    dot_general x22, matrix products, mix_blocks(): jnp.einsum('lij,ljc->lic', weights[:, 1], partner, preferred_element_type...  154 us
    unnamed x104, local copies, waits for them, and re-layouts  153 us
    dot_general x22, matrix products, mix_blocks(): jnp.einsum('lij,ljc->lic', weights[:, 0], act_blocks, preferred_element_t...  100 us
    rev x16, local copies, waits for them, and re-layouts, local_partner(): return grouped[:, ::-1].reshape(act_blocks.shape)  76.8 us
  transfers between devices with their start and end apart: 6, of which 4 were waited for; matrix products, arithmetic and copies ran while one was open for 24% of the time, Pallas kernels for 0%

commit v1 on v0

v1 whole, which is shorter than its diff:
```python
import functools

import jax
import jax.numpy as jnp
from jax import lax
from jax.experimental import pallas as pl
from jax.experimental.pallas import tpu as pltpu
from jax.sharding import PartitionSpec as P

MESH = pl.DeviceIdType.MESH
BF = jnp.bfloat16
F32 = jnp.float32
LANES = 128


def spread(w):
    br = w.shape[0]
    fold = LANES // br
    lane = lax.broadcasted_iota(jnp.int32, w.shape, 1) // br
    zero = jnp.zeros_like(w)
    return jnp.concatenate([jnp.where(lane == k, w, zero) for k in range(fold)], axis=0)


def pair_tile(za, zb, wa, wb):
    top = jnp.concatenate([spread(wa[0]), spread(wa[1])], axis=1)
    low = jnp.concatenate([spread(wb[1]), spread(wb[0])], axis=1)
    lhs = jnp.concatenate([top, low], axis=0)
    rhs = jnp.concatenate([za, zb], axis=0)
    out = jnp.dot(lhs, rhs, preferred_element_type=F32)
    rows = za.shape[0]
    return out[:rows], out[rows:]


def own_tile(own, other, w):
    lhs = jnp.concatenate([spread(w[0]), spread(w[1])], axis=1)
    return jnp.dot(lhs, jnp.concatenate([own, other], axis=0), preferred_element_type=F32)


def swap_rows(z, dist, br):
    n = z.shape[0] // br
    return jnp.concatenate([z[(k ^ dist) * br:((k ^ dist) + 1) * br] for k in range(n)], axis=0)


def radix4(zs, ws, order):
    zs = list(zs)
    for stage, dist in enumerate(order):
        new = [None] * 4
        for a in range(4):
            b = a ^ dist
            if a < b:
                oa, ob = pair_tile(zs[a], zs[b], ws[stage][a], ws[stage][b])
                new[a], new[b] = oa.astype(BF), ob.astype(BF)
        zs = new
    return zs


def gelu(x):
    return 0.5 * x * (1.0 + lax.erf(x * 0.7071067811865476))


def kernel(chips, sig, w1t, w1l, w2l, w2t, out,
           t1, z2, zs1, zm, zs2, t2, wl, wt,
           a1s, a1r, p1s, p1r, a2s, a2r, p2s, p2r, d1s, d1r, d2s, d2r, a3s, a3r, a4s, a4r,
           lsem, wsem, osem):
    d = lax.axis_index("sp")
    x = d // 2
    c = d % 2
    sib = x * 2 + (1 - c)
    br = wl.shape[3]
    gr = LANES // br * br
    nk = z2.shape[0]
    no = z2.shape[2] // gr
    ch = z2.shape[2]

    def peer(r):
        return (x + r) % chips

    def dev(q):
        return {"sp": q * 2 + c}

    barrier = pltpu.get_barrier_semaphore()
    for r in range(1, chips):
        pl.semaphore_signal(barrier, inc=1, device_id=dev(peer(r)), device_id_type=MESH)
    pl.semaphore_signal(barrier, inc=1, device_id={"sp": sib}, device_id_type=MESH)

    def rows_of(q, k):
        return pl.ds(pl.multiple_of((q * nk + k) * ch, ch), ch)

    def load_w(i):
        src = w1l.at[i] if i < w1l.shape[0] else w2l.at[i - w1l.shape[0]]
        return pltpu.make_async_copy(src, wl.at[i], wsem.at[i])

    def own_a1(k):
        return pltpu.make_async_copy(sig.at[rows_of(x, k)], t1.at[k, x], lsem.at[k])

    def wt_rows(q, k):
        return pl.ds((q * nk + k) * no, no)

    def own_p1(k):
        return pltpu.make_async_copy(w1t.at[wt_rows(x, k)], wt.at[0, k, x], lsem.at[nk + k])

    def own_p2(k):
        return pltpu.make_async_copy(w2t.at[wt_rows(x, k)], wt.at[1, k, x], lsem.at[2 * nk + k])

    for k in range(nk):
        own_a1(k).start()
        own_p1(k).start()
    for i in range(wl.shape[0]):
        load_w(i).start()
    for k in range(nk):
        own_p2(k).start()
    pl.semaphore_wait(barrier, chips)

    def slot(k, r):
        return k * (chips - 1) + (r - 1)

    def remote(src, dst, ss, rs, i, q):
        return pltpu.make_async_remote_copy(src, dst, ss.at[i], rs.at[i], device_id=dev(q), device_id_type=MESH)

    def a1(k, r):
        return remote(sig.at[rows_of(peer(r), k)], t1.at[k, x], a1s, a1r, slot(k, r), peer(r))

    def p1(k, r):
        return remote(w1t.at[wt_rows(peer(r), k)], wt.at[0, k, x], p1s, p1r, slot(k, r), peer(r))

    def a2(k, r):
        return remote(t1.at[k, peer(r)], z2.at[k, x], a2s, a2r, slot(k, r), peer(r))

    def p2(k, r):
        return remote(w2t.at[wt_rows(peer(r), k)], wt.at[1, k, x], p2s, p2r, slot(k, r), peer(r))

    def a3(k, r):
        return remote(t1.at[k, peer(r)], t2.at[k, x], a3s, a3r, slot(k, r), peer(r))

    def a4(k, r):
        return remote(t2.at[k, peer(r)], out.at[rows_of(x, k)], a4s, a4r, slot(k, r), peer(r))

    def d1(k):
        return pltpu.make_async_remote_copy(z2.at[k], zs1.at[k], d1s.at[k], d1r.at[k], device_id={"sp": sib}, device_id_type=MESH)

    def d2(k):
        return pltpu.make_async_remote_copy(zm.at[k], zs2.at[k], d2s.at[k], d2r.at[k], device_id={"sp": sib}, device_id_type=MESH)

    def own_a2(k):
        return pltpu.make_async_copy(t1.at[k, x], z2.at[k, x], osem.at[k])

    def own_a3(k):
        return pltpu.make_async_copy(t1.at[k, x], t2.at[k, x], osem.at[nk + k])

    def own_a4(k):
        return pltpu.make_async_copy(t2.at[k, x], out.at[rows_of(x, k)], osem.at[2 * nk + k])

    for k in range(nk):
        for r in range(1, chips):
            p1(k, r).start()
            a1(k, r).start()

    def grp(o):
        return pl.ds(o * gr, gr)

    def gidx(k, q, o):
        return (q * nk + k) * no + o

    def t_stage(buf, m, k, order):
        for o in range(no):
            ws = [[(wt[m, k, p, o, s, 0], wt[m, k, p, o, s, 1]) for p in range(chips)] for s in range(2)]
            zs = radix4([buf[k, p, grp(o), :] for p in range(chips)], ws, order)
            for p in range(chips):
                buf[k, p, grp(o), :] = zs[p]

    @pl.loop(0, nk)
    def _(k):
        own_a1(k).wait()
        own_p1(k).wait()
        for r in range(1, chips):
            p1(k, r).wait_recv()
            a1(k, r).wait_recv()
        t_stage(t1, 0, k, (2, 1))
        own_a2(k).start()
        for r in range(1, chips):
            a2(k, r).start()

    for k in range(nk):
        for r in range(1, chips):
            p2(k, r).start()
    for i in range(wl.shape[0]):
        load_w(i).wait()

    def wpair(i, g):
        return wl[i, g, 0], wl[i, g, 1]

    @pl.loop(0, nk)
    def _(k):
        own_a2(k).wait()
        for r in range(1, chips):
            a2(k, r).wait_recv()
        d1(k).start()

    @pl.loop(0, nk)
    def _(k):
        d1(k).wait_recv()
        for o in range(no):
            zs = []
            for q in range(chips):
                g = gidx(k, q, o)
                zs.append(own_tile(z2[k, q, grp(o), :], zs1[k, q, grp(o), :], wpair(0, g)).astype(BF))
            ws = [[wpair(1 + s, gidx(k, q, o)) for q in range(chips)] for s in range(2)]
            zs = radix4(zs, ws, (2, 1))
            for q in range(chips):
                zm[k, q, grp(o), :] = zs[q]

    def pass_k(first, order):
        @pl.loop(0, chips)
        def _(q):
            for o in range(no):
                ws = [[wpair(first + s, gidx(k, q, o)) for k in range(nk)] for s in range(2)]
                zs = radix4([zm[k, q, grp(o), :] for k in range(nk)], ws, order)
                for k in range(nk):
                    zm[k, q, grp(o), :] = zs[k]

    def pass_o(first, order):
        @pl.loop(0, nk)
        def _(k):
            for q in range(chips):
                ws = [[wpair(first + s, gidx(k, q, o)) for o in range(no)] for s in range(2)]
                zs = radix4([zm[k, q, grp(o), :] for o in range(no)], ws, order)
                for o in range(no):
                    zm[k, q, grp(o), :] = zs[o]

    pass_k(3, (2, 1))
    pass_o(5, (2, 1))

    @pl.loop(0, nk)
    def _(k):
        @pl.loop(0, chips)
        def _(q):
            zs = [zm[k, q, grp(o), :] for o in range(no)]
            gs = [gidx(k, q, o) for o in range(no)]
            zs = [own_tile(z, swap_rows(z, 2, br), wpair(7, g)).astype(BF) for z, g in zip(zs, gs)]
            zs = [own_tile(z, swap_rows(z, 1, br), wpair(8, g)).astype(BF) for z, g in zip(zs, gs)]
            zs = [gelu(z.astype(F32)).astype(BF) for z in zs]
            zs = [own_tile(z, swap_rows(z, 1, br), wpair(9, g)).astype(BF) for z, g in zip(zs, gs)]
            zs = [own_tile(z, swap_rows(z, 2, br), wpair(10, g)).astype(BF) for z, g in zip(zs, gs)]
            for o in range(no):
                zm[k, q, grp(o), :] = zs[o]

    pass_o(11, (1, 2))
    pass_k(13, (1, 2))

    for k in range(nk):
        for r in range(1, chips):
            a1(k, r).wait_send()
            p1(k, r).wait_send()
            a2(k, r).wait_send()

    @pl.loop(0, nk)
    def _(k):
        for o in range(no):
            ws = [[wpair(15 + s, gidx(k, q, o)) for q in range(chips)] for s in range(2)]
            zs = radix4([zm[k, q, grp(o), :] for q in range(chips)], ws, (1, 2))
            for q in range(chips):
                zm[k, q, grp(o), :] = zs[q]
        d2(k).start()

    @pl.loop(0, nk)
    def _(k):
        d2(k).wait_recv()
        for o in range(no):
            for q in range(chips):
                z = own_tile(zm[k, q, grp(o), :], zs2[k, q, grp(o), :], wpair(17, gidx(k, q, o)))
                t1[k, q, grp(o), :] = z.astype(BF)
        own_a3(k).start()
        for r in range(1, chips):
            a3(k, r).start()

    @pl.loop(0, nk)
    def _(k):
        own_a3(k).wait()
        own_p2(k).wait()
        for r in range(1, chips):
            p2(k, r).wait_recv()
            a3(k, r).wait_recv()
        t_stage(t2, 1, k, (1, 2))
        own_a4(k).start()
        for r in range(1, chips):
            a4(k, r).start()

    @pl.loop(0, nk)
    def _(k):
        own_a4(k).wait()
        d1(k).wait_send()
        d2(k).wait_send()
        for r in range(1, chips):
            a4(k, r).wait_recv()
            p2(k, r).wait_send()
            a3(k, r).wait_send()
            a4(k, r).wait_send()


def solution(mesh):
    chips = mesh.shape["sp"] // 2

    def prep(w):
        st, nb, two, br, _ = w.shape
        fold = LANES // br
        w = w.reshape(st, nb // fold, fold, two, br, br)
        return w.transpose(0, 1, 3, 4, 2, 5).reshape(st, nb // fold, two, br, LANES)

    def device_program(signal, w_first, w_second):
        rows, cols = signal.shape
        st, nb, two, br, _ = w_first.shape
        fold = LANES // br
        nk = 4
        ch = rows // (chips * nk)
        no = ch // (fold * br)
        w1 = prep(w_first)
        w2 = prep(w_second)
        w1t, w1l = w1[:2].transpose(1, 0, 2, 3, 4), w1[2:]
        w2l, w2t = w2[:st - 2], w2[st - 2:].transpose(1, 0, 2, 3, 4)
        buf = pltpu.VMEM((nk, chips, ch, cols), BF)
        ns = nk * (chips - 1)
        pairs = [ns, ns, ns, ns, nk, nk, ns, ns]
        sems = [pltpu.SemaphoreType.DMA((n,)) for n in pairs for _ in range(2)]
        hbm = pl.BlockSpec(memory_space=pl.ANY)
        return pl.pallas_call(
            functools.partial(kernel, chips),
            out_shape=jax.ShapeDtypeStruct((rows, cols), BF),
            in_specs=[hbm] * 5,
            out_specs=hbm,
            scratch_shapes=[
                buf, buf, buf, buf, buf, buf,
                pltpu.VMEM((2 * (st - 2), nb // fold, two, br, LANES), BF),
                pltpu.VMEM((2, nk, chips, no, 2, two, br, LANES), BF),
                *sems,
                pltpu.SemaphoreType.DMA((3 * nk,)),
                pltpu.SemaphoreType.DMA((2 * (st - 2),)),
                pltpu.SemaphoreType.DMA((3 * nk,)),
            ],
            compiler_params=pltpu.CompilerParams(
                collective_id=0, has_side_effects=True, vmem_limit_bytes=60 * 2**20
            ),
        )(signal, w1t, w1l, w2l, w2t)

    row_spec = P(("dp", "sp"), None)
    weight_spec = P(None, "sp", None, None, None)
    return jax.shard_map(device_program, mesh=mesh, in_specs=(row_spec, weight_spec, weight_spec), out_specs=row_spec, check_vma=False)
```

time: 831 us -> 641 us (0.77)
  waiting for transfers between devices: 306 us -> 0 us
  Pallas kernels: 0 us -> 259 us
  matrix products: 254 us -> 0 us
  local copies, waits for them, and re-layouts: 246 us -> 377 us
  starting transfers between devices: 12.8 us -> 0 us
    ppermute x6 -> x0, waiting for transfers between devices: 306 us -> none  [apply_map(): partner = lax.ppermute(act_blocks, 'sp', pairing)]
    pallas_call x0 -> x1, Pallas kernels: none -> 259 us  [device_program(): pl.pallas_call(functools.partial(kernel, chips), out_shape=jax.ShapeDtype...]
    dot_general x44 -> x0, matrix products: 254 us -> none  [the longest x22 154 us: mix_blocks(): jnp.einsum('lij,ljc->lic', weights[:, 1], partner, preferred_element_type...]
    slice x2 -> x12, local copies, waits for them, and re-layouts: 16.1 us -> 252 us  [the longest x6 126 us: device_program(): w2l, w2t = (w2[:st - 2], w2[st - 2:].transpose(1, 0, 2, 3, 4))]
    rev x16 -> x0, local copies, waits for them, and re-layouts: 76.8 us -> none  [local_partner(): return grouped[:, ::-1].reshape(act_blocks.shape)]
    unnamed x104 -> x3, local copies, waits for them, and re-layouts: 153 us -> 125 us
    ppermute x6 -> x0, starting transfers between devices: 12.8 us -> none  [apply_map(): partner = lax.ppermute(act_blocks, 'sp', pairing)]
  transfers between devices with their start and end apart: 6 -> 0, of which waited for: 4 -> 0; matrix products, arithmetic and copies ran while one was open for 24% -> 0% of each run, Pallas kernels for 0% -> 0%
where the time goes in v1:
time: 641 us; the launch traced here: 636 us
  local copies, waits for them, and re-layouts  377 us (59%)
  Pallas kernels  259 us (40%)
    pallas_call x1, Pallas kernels, device_program(): pl.pallas_call(functools.partial(kernel, chips), out_shape=jax.ShapeDtype...  259 us
    slice x6, local copies, waits for them, and re-layouts, device_program(): w2l, w2t = (w2[:st - 2], w2[st - 2:].transpose(1, 0, 2, 3, 4))  126 us
    slice x6, local copies, waits for them, and re-layouts, device_program(): w1t, w1l = (w1[:2].transpose(1, 0, 2, 3, 4), w1[2:])  126 us
    unnamed x3, local copies, waits for them, and re-layouts  125 us

profile of v1, /device:TPU:81, one launch (start us, length us, event | category | flops | bytes accessed | tf_op | source)
XLA Modules:
  0.0 635.7 jit_solution(11705460592971601419)
XLA Ops:
  0.0 60.2 %copy.8 = bf16[11,256,2,32,32]{4,3,2,1,0:T(8,128)(2,1)} copy(bf16[11,256,2,32,32]{1,4,3,2,0:T(8,128)(2,1)} %param.4) | data formatting | bytes 23068672 | tf_op args[1]
  60.2 10.5 %slice.32 = bf16[2,64,2,32,4,32]{5,3,2,4,1,0:T(8,128)(2,1)} slice(bf16[11,64,2,32,4,32]{5,3,2,4,1,0:T(8,128)(2,1)} %bitcast.12), slice={[0:2], [0:64], [0:2], [0:32], [0:4], [0:32]} | slice | bytes 4194304 | tf_op jit(solution)/shard_map/slice | solution.py:318
  70.7 25.8 %slice.33 = bf16[9,64,2,32,4,32]{5,3,2,4,1,0:T(8,128)(2,1)} slice(bf16[11,64,2,32,4,32]{5,3,2,4,1,0:T(8,128)(2,1)} %bitcast.13), slice={[2:11], [0:64], [0:2], [0:32], [0:4], [0:32]} | slice | bytes 18874368 | tf_op jit(solution)/shard_map/slice | solution.py:318
  96.4 50.3 %copy.11 = bf16[9,64,2,32,4,32]{1,5,4,3,2,0:T(8,128)(2,1)} copy(bf16[9,64,2,32,4,32]{5,3,2,4,1,0:T(8,128)(2,1)} %slice.33) | data formatting | bytes 18874368 | tf_op jit(solution)/shard_map/slice | solution.py:318
  146.7 12.6 %copy.9 = bf16[2,64,2,32,4,32]{1,5,4,3,2,0:T(8,128)(2,1)} copy(bf16[2,64,2,32,4,32]{5,3,2,4,1,0:T(8,128)(2,1)} %slice.32) | data formatting | bytes 4194304 | tf_op jit(solution)/shard_map/slice | solution.py:318
  159.3 5.7 copy.10
  165.0 21.0 %copy.16.w1l = bf16[9,64,2,32,128]{4,3,2,1,0:T(8,128)(2,1)} copy(bf16[9,64,2,32,128]{1,4,3,2,0:T(8,128)(2,1)} %bitcast.16) | data formatting | bytes 18874368 | tf_op jit(solution)/shard_map/slice | solution.py:318
  185.9 60.2 %copy.12 = bf16[11,256,2,32,32]{4,3,2,1,0:T(8,128)(2,1)} copy(bf16[11,256,2,32,32]{1,4,3,2,0:T(8,128)(2,1)} %param.5) | data formatting | bytes 23068672 | tf_op args[2]
  246.1 10.6 %slice.35 = bf16[2,64,2,32,4,32]{5,3,2,4,1,0:T(8,128)(2,1)} slice(bf16[11,64,2,32,4,32]{5,3,2,4,1,0:T(8,128)(2,1)} %bitcast.14), slice={[9:11], [0:64], [0:2], [0:32], [0:4], [0:32]} | slice | bytes 4194304 | tf_op jit(solution)/shard_map/slice | solution.py:319
  256.7 25.8 %slice.34 = bf16[9,64,2,32,4,32]{5,3,2,4,1,0:T(8,128)(2,1)} slice(bf16[11,64,2,32,4,32]{5,3,2,4,1,0:T(8,128)(2,1)} %bitcast.15), slice={[0:9], [0:64], [0:2], [0:32], [0:4], [0:32]} | slice | bytes 18874368 | tf_op jit(solution)/shard_map/slice | solution.py:319
  282.5 50.5 %copy.13 = bf16[9,64,2,32,4,32]{1,5,4,3,2,0:T(8,128)(2,1)} copy(bf16[9,64,2,32,4,32]{5,3,2,4,1,0:T(8,128)(2,1)} %slice.34) | data formatting | bytes 18874368 | tf_op jit(solution)/shard_map/slice | solution.py:319
  333.0 12.6 %copy.14 = bf16[2,64,2,32,4,32]{1,5,4,3,2,0:T(8,128)(2,1)} copy(bf16[2,64,2,32,4,32]{5,3,2,4,1,0:T(8,128)(2,1)} %slice.35) | data formatting | bytes 4194304 | tf_op jit(solution)/shard_map/slice | solution.py:319
  345.6 5.7 copy.15
  351.2 20.9 %copy.17.w2l = bf16[9,64,2,32,128]{4,3,2,1,0:T(8,128)(2,1)} copy(bf16[9,64,2,32,128]{1,4,3,2,0:T(8,128)(2,1)} %bitcast.17) | data formatting | bytes 18874368 | tf_op jit(solution)/shard_map/slice | solution.py:319
  372.2 259.1 %shard_map.37 = bf16[8192,256]{1,0:T(8,128)(2,1)} custom-call(bf16[8192,256]{1,0:T(8,128)(2,1)} %sig.1, bf16[64,2,2,32,128]{4,3,2,1,0:T(8,128)(2,1)} %bitcast.20, bf16[9,64,2,32,128]{4,3,2,1,0:T(8,128)(2,1)} %copy.16.w1l, bf16[9,64,2,32,128]{4,3,2,1,0:T(8,128)(2,1)} %copy.17.w2l, bf16[64,2,2,32,128]{4,3,2,1,0:T(8,128)(2,1)} %bitcast.21), custom_call_target="tpu_custom_call" | custom-call | tf_op jit(solution)/shard_map/pallas_call | solution.py:325
  631.3 4.5 copy.19

commit v2 on v1

--- a/solution.py
+++ b/solution.py
@@ -58,8 +58,36 @@
     return 0.5 * x * (1.0 + lax.erf(x * 0.7071067811865476))
 
 
-def kernel(chips, sig, w1t, w1l, w2l, w2t, out,
-           t1, z2, zs1, zm, zs2, t2, wl, wt,
+def prep_stage(raw, mid, perm, sel, dst):
+    two, br, _, nb = raw.shape
+    fold = LANES // br
+    lane = lax.broadcasted_iota(jnp.int32, (br, nb), 1) % fold
+    zero = jnp.zeros((br, nb), BF)
+    tile = perm.shape[0] // 16
+    unroll = 8
+
+    @pl.loop(0, br // unroll)
+    def _(h):
+        for u in range(unroll):
+            i = h * unroll + u
+            rhs = jnp.concatenate([jnp.where(lane == k, raw[t, i], zero) for t in range(two) for k in range(fold)], axis=0)
+            y = lax.dot_general(sel[...], rhs, (((1,), (1,)), ((), ())), preferred_element_type=F32)
+            mid[i] = y.astype(BF)
+
+    @pl.loop(0, nb // fold // tile // 2)
+    def _(h):
+        for u in range(2):
+            g0 = (h * 2 + u) * tile
+            for half in range(br // 16):
+                rhs = jnp.concatenate([mid[half * 16 + v, pl.ds(pl.multiple_of(g0, tile), tile), :] for v in range(16)], axis=0)
+                res = jnp.dot(perm[...], rhs, preferred_element_type=F32).astype(BF)
+                for g in range(tile):
+                    for t in range(two):
+                        dst[g0 + g, t, half * 16:(half + 1) * 16, :] = res[g * 16:(g + 1) * 16, t * LANES:(t + 1) * LANES]
+
+
+def kernel(chips, sig, w1, w2, out,
+           t1, z2, zs1, zm, zs2, t2, wl, wt, raw, mid, perm, sel,
            a1s, a1r, p1s, p1r, a2s, a2r, p2s, p2r, d1s, d1r, d2s, d2r, a3s, a3r, a4s, a4r,
            lsem, wsem, osem):
     d = lax.axis_index("sp")
@@ -86,9 +114,29 @@
     def rows_of(q, k):
         return pl.ds(pl.multiple_of((q * nk + k) * ch, ch), ch)
 
-    def load_w(i):
-        src = w1l.at[i] if i < w1l.shape[0] else w2l.at[i - w1l.shape[0]]
-        return pltpu.make_async_copy(src, wl.at[i], wsem.at[i])
+    st = w1.shape[0]
+
+    two = wl.shape[2]
+    last = 2 * st - 1
+
+    def load_w(w, stage, n):
+        return pltpu.make_async_copy(w.at[stage], raw.at[n % 2], wsem.at[n % 2])
+
+    def load_job(n):
+        @pl.when(n < st)
+        def _():
+            load_w(w1, n, n).start()
+
+        @pl.when((n >= st) & (n <= last))
+        def _():
+            load_w(w2, (n - 2) % st, n).start()
+
+    def jobs(lo, hi):
+        @pl.loop(lo, hi)
+        def _(n):
+            load_job(n + 1)
+            load_w(w1, 0, n).wait()
+            prep_stage(raw.at[n % 2], mid, perm, sel, wl.at[n])
 
     def own_a1(k):
         return pltpu.make_async_copy(sig.at[rows_of(x, k)], t1.at[k, x], lsem.at[k])
@@ -97,18 +145,21 @@
         return pl.ds((q * nk + k) * no, no)
 
     def own_p1(k):
-        return pltpu.make_async_copy(w1t.at[wt_rows(x, k)], wt.at[0, k, x], lsem.at[nk + k])
+        return pltpu.make_async_copy(wl.at[pl.ds(0, 2), wt_rows(x, k)], wt.at[0, k, x], lsem.at[nk + k])
 
     def own_p2(k):
-        return pltpu.make_async_copy(w2t.at[wt_rows(x, k)], wt.at[1, k, x], lsem.at[2 * nk + k])
-
+        return pltpu.make_async_copy(wl.at[pl.ds(st, 2), wt_rows(x, k)], wt.at[1, k, x], lsem.at[2 * nk + k])
+
+    load_w(w1, 0, 0).start()
     for k in range(nk):
         own_a1(k).start()
-        own_p1(k).start()
-    for i in range(wl.shape[0]):
-        load_w(i).start()
-    for k in range(nk):
-        own_p2(k).start()
+    row = lax.broadcasted_iota(jnp.int32, perm.shape, 0)
+    col = lax.broadcasted_iota(jnp.int32, perm.shape, 1)
+    tile = perm.shape[0] // 16
+    perm[...] = (col == row % 16 * tile + row // 16).astype(F32).astype(BF)
+    row = lax.broadcasted_iota(jnp.int32, sel.shape, 0)
+    col = lax.broadcasted_iota(jnp.int32, sel.shape, 1)
+    sel[...] = (row == col // (LANES // br)).astype(F32).astype(BF)
     pl.semaphore_wait(barrier, chips)
 
     def slot(k, r):
@@ -121,13 +172,13 @@
         return remote(sig.at[rows_of(peer(r), k)], t1.at[k, x], a1s, a1r, slot(k, r), peer(r))
 
     def p1(k, r):
-        return remote(w1t.at[wt_rows(peer(r), k)], wt.at[0, k, x], p1s, p1r, slot(k, r), peer(r))
+        return remote(wl.at[pl.ds(0, 2), wt_rows(peer(r), k)], wt.at[0, k, x], p1s, p1r, slot(k, r), peer(r))
 
     def a2(k, r):
         return remote(t1.at[k, peer(r)], z2.at[k, x], a2s, a2r, slot(k, r), peer(r))
 
     def p2(k, r):
-        return remote(w2t.at[wt_rows(peer(r), k)], wt.at[1, k, x], p2s, p2r, slot(k, r), peer(r))
+        return remote(wl.at[pl.ds(st, 2), wt_rows(peer(r), k)], wt.at[1, k, x], p2s, p2r, slot(k, r), peer(r))
 
     def a3(k, r):
         return remote(t1.at[k, peer(r)], t2.at[k, x], a3s, a3r, slot(k, r), peer(r))
@@ -150,10 +201,23 @@
     def own_a4(k):
         return pltpu.make_async_copy(t2.at[k, x], out.at[rows_of(x, k)], osem.at[2 * nk + k])
 
-    for k in range(nk):
+    def send_a1(k):
+        for r in range(1, chips):
+            a1(k, r).start()
+
+    def send_p1(k):
+        own_p1(k).start()
         for r in range(1, chips):
             p1(k, r).start()
-            a1(k, r).start()
+
+    send_a1(0)
+    send_a1(1)
+    jobs(0, 2)
+    send_p1(0)
+    send_p1(1)
+    for k in range(2, nk):
+        send_a1(k)
+        send_p1(k)
 
     def grp(o):
         return pl.ds(o * gr, gr)
@@ -163,13 +227,14 @@
 
     def t_stage(buf, m, k, order):
         for o in range(no):
-            ws = [[(wt[m, k, p, o, s, 0], wt[m, k, p, o, s, 1]) for p in range(chips)] for s in range(2)]
+            ws = [[(wt[m, k, p, s, o, 0], wt[m, k, p, s, o, 1]) for p in range(chips)] for s in range(2)]
             zs = radix4([buf[k, p, grp(o), :] for p in range(chips)], ws, order)
             for p in range(chips):
                 buf[k, p, grp(o), :] = zs[p]
 
     @pl.loop(0, nk)
     def _(k):
+        jobs(2 + 4 * k, 6 + 4 * k)
         own_a1(k).wait()
         own_p1(k).wait()
         for r in range(1, chips):
@@ -181,10 +246,10 @@
             a2(k, r).start()
 
     for k in range(nk):
+        own_p2(k).start()
         for r in range(1, chips):
             p2(k, r).start()
-    for i in range(wl.shape[0]):
-        load_w(i).wait()
+    jobs(2 + 4 * nk, 2 * st)
 
     def wpair(i, g):
         return wl[i, g, 0], wl[i, g, 1]
@@ -203,8 +268,8 @@
             zs = []
             for q in range(chips):
                 g = gidx(k, q, o)
-                zs.append(own_tile(z2[k, q, grp(o), :], zs1[k, q, grp(o), :], wpair(0, g)).astype(BF))
-            ws = [[wpair(1 + s, gidx(k, q, o)) for q in range(chips)] for s in range(2)]
+                zs.append(own_tile(z2[k, q, grp(o), :], zs1[k, q, grp(o), :], wpair(2, g)).astype(BF))
+            ws = [[wpair(3 + s, gidx(k, q, o)) for q in range(chips)] for s in range(2)]
             zs = radix4(zs, ws, (2, 1))
             for q in range(chips):
                 zm[k, q, grp(o), :] = zs[q]
@@ -227,8 +292,8 @@
                 for o in range(no):
                     zm[k, q, grp(o), :] = zs[o]
 
-    pass_k(3, (2, 1))
-    pass_o(5, (2, 1))
+    pass_k(5, (2, 1))
+    pass_o(7, (2, 1))
 
     @pl.loop(0, nk)
     def _(k):
@@ -236,16 +301,16 @@
         def _(q):
             zs = [zm[k, q, grp(o), :] for o in range(no)]
             gs = [gidx(k, q, o) for o in range(no)]
-            zs = [own_tile(z, swap_rows(z, 2, br), wpair(7, g)).astype(BF) for z, g in zip(zs, gs)]
-            zs = [own_tile(z, swap_rows(z, 1, br), wpair(8, g)).astype(BF) for z, g in zip(zs, gs)]
+            zs = [own_tile(z, swap_rows(z, 2, br), wpair(9, g)).astype(BF) for z, g in zip(zs, gs)]
+            zs = [own_tile(z, swap_rows(z, 1, br), wpair(10, g)).astype(BF) for z, g in zip(zs, gs)]
             zs = [gelu(z.astype(F32)).astype(BF) for z in zs]
-            zs = [own_tile(z, swap_rows(z, 1, br), wpair(9, g)).astype(BF) for z, g in zip(zs, gs)]
-            zs = [own_tile(z, swap_rows(z, 2, br), wpair(10, g)).astype(BF) for z, g in zip(zs, gs)]
+            zs = [own_tile(z, swap_rows(z, 1, br), wpair(st + 2, g)).astype(BF) for z, g in zip(zs, gs)]
+            zs = [own_tile(z, swap_rows(z, 2, br), wpair(st + 3, g)).astype(BF) for z, g in zip(zs, gs)]
             for o in range(no):
                 zm[k, q, grp(o), :] = zs[o]
 
-    pass_o(11, (1, 2))
-    pass_k(13, (1, 2))
+    pass_o(st + 4, (1, 2))
+    pass_k(st + 6, (1, 2))
 
     for k in range(nk):
         for r in range(1, chips):
@@ -256,7 +321,7 @@
     @pl.loop(0, nk)
     def _(k):
         for o in range(no):
-            ws = [[wpair(15 + s, gidx(k, q, o)) for q in range(chips)] for s in range(2)]
+            ws = [[wpair(st + 8 + s, gidx(k, q, o)) for q in range(chips)] for s in range(2)]
             zs = radix4([zm[k, q, grp(o), :] for q in range(chips)], ws, (1, 2))
             for q in range(chips):
                 zm[k, q, grp(o), :] = zs[q]
@@ -267,7 +332,7 @@
         d2(k).wait_recv()
         for o in range(no):
             for q in range(chips):
-                z = own_tile(zm[k, q, grp(o), :], zs2[k, q, grp(o), :], wpair(17, gidx(k, q, o)))
+                z = own_tile(zm[k, q, grp(o), :], zs2[k, q, grp(o), :], wpair(st + 10, gidx(k, q, o)))
                 t1[k, q, grp(o), :] = z.astype(BF)
         own_a3(k).start()
         for r in range(1, chips):
@@ -299,12 +364,6 @@
 
 def solution(mesh):
     chips = mesh.shape["sp"] // 2
-
-    def prep(w):
-        st, nb, two, br, _ = w.shape
-        fold = LANES // br
-        w = w.reshape(st, nb // fold, fold, two, br, br)
-        return w.transpose(0, 1, 3, 4, 2, 5).reshape(st, nb // fold, two, br, LANES)
 
     def device_program(signal, w_first, w_second):
         rows, cols = signal.shape
@@ -313,10 +372,8 @@
         nk = 4
         ch = rows // (chips * nk)
         no = ch // (fold * br)
-        w1 = prep(w_first)
-        w2 = prep(w_second)
-        w1t, w1l = w1[:2].transpose(1, 0, 2, 3, 4), w1[2:]
-        w2l, w2t = w2[:st - 2], w2[st - 2:].transpose(1, 0, 2, 3, 4)
+        w1 = w_first.transpose(0, 2, 3, 4, 1)
+        w2 = w_second.transpose(0, 2, 3, 4, 1)
         buf = pltpu.VMEM((nk, chips, ch, cols), BF)
         ns = nk * (chips - 1)
         pairs = [ns, ns, ns, ns, nk, nk, ns, ns]
@@ -325,21 +382,25 @@
         return pl.pallas_call(
             functools.partial(kernel, chips),
             out_shape=jax.ShapeDtypeStruct((rows, cols), BF),
-            in_specs=[hbm] * 5,
+            in_specs=[hbm] * 3,
             out_specs=hbm,
             scratch_shapes=[
                 buf, buf, buf, buf, buf, buf,
-                pltpu.VMEM((2 * (st - 2), nb // fold, two, br, LANES), BF),
-                pltpu.VMEM((2, nk, chips, no, 2, two, br, LANES), BF),
+                pltpu.VMEM((2 * st, nb // fold, two, br, LANES), BF),
+                pltpu.VMEM((2, nk, chips, 2, no, two, br, LANES), BF),
+                pltpu.VMEM((2, two, br, br, nb), BF),
+                pltpu.VMEM((br, nb // fold, two * LANES), BF),
+                pltpu.VMEM((nb, nb), BF),
+                pltpu.VMEM((nb // fold, nb), BF),
                 *sems,
                 pltpu.SemaphoreType.DMA((3 * nk,)),
-                pltpu.SemaphoreType.DMA((2 * (st - 2),)),
+                pltpu.SemaphoreType.DMA((2,)),
                 pltpu.SemaphoreType.DMA((3 * nk,)),
             ],
             compiler_params=pltpu.CompilerParams(
                 collective_id=0, has_side_effects=True, vmem_limit_bytes=60 * 2**20
             ),
-        )(signal, w1t, w1l, w2l, w2t)
+        )(signal, w1, w2)
 
     row_spec = P(("dp", "sp"), None)
     weight_spec = P(None, "sp", None, None, None)

time: 641 us -> 264 us (0.41)
  local copies, waits for them, and re-layouts: 377 us -> 4.47 us
    slice x12 -> x0, local copies, waits for them, and re-layouts: 252 us -> none  [the longest x6 126 us: device_program(): w2l, w2t = (w2[:st - 2], w2[st - 2:].transpose(1, 0, 2, 3, 4))]
    unnamed x3 -> x1, local copies, waits for them, and re-layouts: 125 us -> 4.47 us
where the time goes in v2:
time: 264 us; the launch traced here: 263 us
  Pallas kernels  259 us (98%)
  local copies, waits for them, and re-layouts  4.47 us (2%)
    pallas_call x1, Pallas kernels, device_program(): pl.pallas_call(functools.partial(kernel, chips), out_shape=jax.ShapeDtype...  259 us

profile of v2, /device:TPU:81, one launch (start us, length us, event | category | flops | bytes accessed | tf_op | source)
XLA Modules:
  0.0 263.2 jit_solution(7339468316042987567)
XLA Ops:
  0.0 258.7 %shard_map.37 = bf16[8192,256]{1,0:T(8,128)(2,1)} custom-call(bf16[8192,256]{1,0:T(8,128)(2,1)} %sig.1, bf16[11,2,32,32,256]{4,3,2,1,0:T(8,128)(2,1)} %bitcast.2, bf16[11,2,32,32,256]{4,3,2,1,0:T(8,128)(2,1)} %bitcast.3), custom_call_target="tpu_custom_call" | custom-call | tf_op jit(solution)/shard_map/pallas_call | solution.py:382
  258.7 4.5 %copy.5 = bf16[8192,256]{1,0:T(8,128)(2,1)} copy(bf16[8192,256]{1,0:T(8,128)(2,1)} %shard_map.37) | data formatting | bytes 8388608

commit v3 on v2

v3 whole, which is shorter than its diff:
```python
import functools

import jax
import jax.numpy as jnp
from jax import lax
from jax.experimental import pallas as pl
from jax.experimental.pallas import tpu as pltpu
from jax.sharding import PartitionSpec as P

MESH = pl.DeviceIdType.MESH
BF = jnp.bfloat16
F32 = jnp.float32
LANES = 128


def lane_masks(shape, br):
    lane = lax.broadcasted_iota(jnp.int32, shape, 1)
    return [(lane >= k * br) & (lane < (k + 1) * br) for k in range(LANES // br)]


def spread(w, masks):
    zero = jnp.zeros_like(w)
    return jnp.concatenate([jnp.where(m, w, zero) for m in masks], axis=0)


def pair_tile(masks, za, zb, wa, wb):
    top = jnp.concatenate([spread(wa[0], masks), spread(wa[1], masks)], axis=1)
    low = jnp.concatenate([spread(wb[1], masks), spread(wb[0], masks)], axis=1)
    lhs = jnp.concatenate([top, low], axis=0)
    rhs = jnp.concatenate([za, zb], axis=0)
    out = jnp.dot(lhs, rhs, preferred_element_type=F32)
    rows = za.shape[0]
    return out[:rows], out[rows:]


def own_tile(masks, own, other, w):
    lhs = jnp.concatenate([spread(w[0], masks), spread(w[1], masks)], axis=1)
    return jnp.dot(lhs, jnp.concatenate([own, other], axis=0), preferred_element_type=F32)


def swap_rows(z, dist, br):
    n = z.shape[0] // br
    return jnp.concatenate([z[(k ^ dist) * br:((k ^ dist) + 1) * br] for k in range(n)], axis=0)


def radix4(masks, zs, ws, order):
    zs = list(zs)
    for stage, dist in enumerate(order):
        new = [None] * 4
        for a in range(4):
            b = a ^ dist
            if a < b:
                oa, ob = pair_tile(masks, zs[a], zs[b], ws[stage][a], ws[stage][b])
                new[a], new[b] = oa.astype(BF), ob.astype(BF)
        zs = new
    return zs


def gelu(x):
    return 0.5 * x * (1.0 + lax.erf(x * 0.7071067811865476))


def prep_stage(nk, raw, mid, perm, sel, dst):
    two, br, _, nb = raw.shape
    fold = LANES // br
    lane = lax.broadcasted_iota(jnp.int32, (br, nb), 1) // nk % fold
    zero = jnp.zeros((br, nb), BF)
    tile = perm.shape[0] // 16
    unroll = 8

    @pl.loop(0, br // unroll)
    def _(h):
        for u in range(unroll):
            i = h * unroll + u
            rhs = jnp.concatenate([jnp.where(lane == k, raw[t, i], zero) for t in range(two) for k in range(fold)], axis=0)
            y = lax.dot_general(sel[...], rhs, (((1,), (1,)), ((), ())), preferred_element_type=F32)
            mid[i] = y.astype(BF)

    @pl.loop(0, nb // fold // tile // 2)
    def _(h):
        for u in range(2):
            g0 = (h * 2 + u) * tile
            for half in range(br // 16):
                rhs = jnp.concatenate([mid[half * 16 + v, pl.ds(pl.multiple_of(g0, tile), tile), :] for v in range(16)], axis=0)
                res = jnp.dot(perm[...], rhs, preferred_element_type=F32).astype(BF)
                for g in range(tile):
                    for t in range(two):
                        dst[g0 + g, t, half * 16:(half + 1) * 16, :] = res[g * 16:(g + 1) * 16, t * LANES:(t + 1) * LANES]


def kernel(chips, sig, w1, w2, out,
           t1, z2, zs1, zm, zs2, t2, wl, wt, raw, mid, perm, sel,
           a1s, a1r, p1s, p1r, a2s, a2r, p2s, p2r, d1s, d1r, d2s, d2r, a3s, a3r, a4s, a4r,
           lsem, wsem, osem):
    d = lax.axis_index("sp")
    x = d // 2
    c = d % 2
    sib = x * 2 + (1 - c)
    br = wl.shape[3]
    fold = LANES // br
    nk = z2.shape[0]
    no = z2.shape[2] // fold

    def peer(r):
        return (x + r) % chips

    def dev(q):
        return {"sp": q * 2 + c}

    barrier = pltpu.get_barrier_semaphore()
    for r in range(1, chips):
        pl.semaphore_signal(barrier, inc=1, device_id=dev(peer(r)), device_id_type=MESH)
    pl.semaphore_signal(barrier, inc=1, device_id={"sp": sib}, device_id_type=MESH)

    st = w1.shape[0]

    two = wl.shape[2]
    last = 2 * st - 1

    def load_w(w, stage, n):
        return pltpu.make_async_copy(w.at[stage], raw.at[n % 2], wsem.at[n % 2])

    def load_job(n):
        @pl.when(n < st)
        def _():
            load_w(w1, n, n).start()

        @pl.when((n >= st) & (n <= last))
        def _():
            load_w(w2, (n - 2) % st, n).start()

    def jobs(lo, hi):
        @pl.loop(lo, hi)
        def _(n):
            load_job(n + 1)
            load_w(w1, 0, n).wait()
            prep_stage(nk, raw.at[n % 2], mid, perm, sel, wl.at[n])

    def own_a1(k):
        return pltpu.make_async_copy(sig.at[x, :, k], t1.at[k, x], lsem.at[k])

    def wt_rows(q, k):
        return pl.ds((q * nk + k) * no, no)

    def own_p1(k):
        return pltpu.make_async_copy(wl.at[pl.ds(0, 2), wt_rows(x, k)], wt.at[0, k, x], lsem.at[nk + k])

    def own_p2(k):
        return pltpu.make_async_copy(wl.at[pl.ds(st, 2), wt_rows(x, k)], wt.at[1, k, x], lsem.at[2 * nk + k])

    load_w(w1, 0, 0).start()
    for k in range(nk):
        own_a1(k).start()
    row = lax.broadcasted_iota(jnp.int32, perm.shape, 0)
    col = lax.broadcasted_iota(jnp.int32, perm.shape, 1)
    tile = perm.shape[0] // 16
    perm[...] = (col == row % 16 * tile + row // 16).astype(F32).astype(BF)
    row = lax.broadcasted_iota(jnp.int32, sel.shape, 0)
    col = lax.broadcasted_iota(jnp.int32, sel.shape, 1)
    span = no * fold * nk
    sel[...] = (row == (col // span * nk + col % nk) * no + col // (fold * nk) % no).astype(F32).astype(BF)
    pl.semaphore_wait(barrier, chips)

    def slot(k, r):
        return k * (chips - 1) + (r - 1)

    def remote(src, dst, ss, rs, i, q):
        return pltpu.make_async_remote_copy(src, dst, ss.at[i], rs.at[i], device_id=dev(q), device_id_type=MESH)

    def a1(k, r):
        return remote(sig.at[peer(r), :, k], t1.at[k, x], a1s, a1r, slot(k, r), peer(r))

    def p1(k, r):
        return remote(wl.at[pl.ds(0, 2), wt_rows(peer(r), k)], wt.at[0, k, x], p1s, p1r, slot(k, r), peer(r))

    def a2(k, r):
        return remote(t1.at[k, peer(r)], z2.at[k, x], a2s, a2r, slot(k, r), peer(r))

    def p2(k, r):
        return remote(wl.at[pl.ds(st, 2), wt_rows(peer(r), k)], wt.at[1, k, x], p2s, p2r, slot(k, r), peer(r))

    def a3(k, r):
        return remote(t1.at[k, peer(r)], t2.at[k, x], a3s, a3r, slot(k, r), peer(r))

    def a4(k, r):
        return remote(t2.at[k, peer(r)], out.at[x, :, k], a4s, a4r, slot(k, r), peer(r))

    def d1(k):
        return pltpu.make_async_remote_copy(z2.at[k], zs1.at[k], d1s.at[k], d1r.at[k], device_id={"sp": sib}, device_id_type=MESH)

    def d2(k):
        return pltpu.make_async_remote_copy(zm.at[k], zs2.at[k], d2s.at[k], d2r.at[k], device_id={"sp": sib}, device_id_type=MESH)

    def own_a2(k):
        return pltpu.make_async_copy(t1.at[k, x], z2.at[k, x], osem.at[k])

    def own_a3(k):
        return pltpu.make_async_copy(t1.at[k, x], t2.at[k, x], osem.at[nk + k])

    def own_a4(k):
        return pltpu.make_async_copy(t2.at[k, x], out.at[x, :, k], osem.at[2 * nk + k])

    def send_a1(k):
        for r in range(1, chips):
            a1(k, r).start()

    def send_p1(k):
        own_p1(k).start()
        for r in range(1, chips):
            p1(k, r).start()

    send_a1(0)
    send_a1(1)
    jobs(0, 2)
    send_p1(0)
    send_p1(1)
    for k in range(2, nk):
        send_a1(k)
        send_p1(k)

    def get(buf, k, q, o):
        return buf[k, q, o * fold:(o + 1) * fold].reshape(fold * br, buf.shape[4])

    def put(buf, k, q, o, z):
        buf[k, q, o * fold:(o + 1) * fold] = z.reshape(fold, br, buf.shape[4])

    masks = lane_masks((br, LANES), br)

    def gidx(k, q, o):
        return (q * nk + k) * no + o

    def t_stage(buf, m, k, order):
        for o in range(no):
            ws = [[(wt[m, k, p, s, o, 0], wt[m, k, p, s, o, 1]) for p in range(chips)] for s in range(2)]
            zs = radix4(masks, [get(buf, k, p, o) for p in range(chips)], ws, order)
            for p in range(chips):
                put(buf, k, p, o, zs[p])

    @pl.loop(0, nk)
    def _(k):
        jobs(2 + 4 * k, 6 + 4 * k)
        own_a1(k).wait()
        own_p1(k).wait()
        for r in range(1, chips):
            p1(k, r).wait_recv()
            a1(k, r).wait_recv()
        t_stage(t1, 0, k, (2, 1))
        own_a2(k).start()
        for r in range(1, chips):
            a2(k, r).start()

    jobs(2 + 4 * nk, 2 * st)

    def wpair(i, g):
        return wl[i, g, 0], wl[i, g, 1]

    def within(zs, gs, i, dist):
        return [own_tile(masks, z, swap_rows(z, dist, br), wpair(i, g)).astype(BF) for z, g in zip(zs, gs)]

    def over_q(k, o, zs, first, order):
        ws = [[wpair(first + s, gidx(k, q, o)) for q in range(chips)] for s in range(2)]
        return radix4(masks, zs, ws, order)

    def over_o(k, q, zs, first, order):
        ws = [[wpair(first + s, gidx(k, q, o)) for o in range(no)] for s in range(2)]
        return radix4(masks, zs, ws, order)

    def far_local(k):
        d1(k).wait_recv()
        for o in range(no):
            zs = [own_tile(masks, get(z2, k, q, o), get(zs1, k, q, o), wpair(2, gidx(k, q, o))).astype(BF) for q in range(chips)]
            for q, z in enumerate(over_q(k, o, zs, 3, (2, 1))):
                put(zm, k, q, o, z)
        for q in range(chips):
            gs = [gidx(k, q, o) for o in range(no)]
            zs = over_o(k, q, [get(zm, k, q, o) for o in range(no)], 5, (2, 1))
            zs = within(within(zs, gs, 7, 2), gs, 8, 1)
            for o in range(no):
                put(zm, k, q, o, zs[o])

    def near_local(k):
        for q in range(chips):
            gs = [gidx(k, q, o) for o in range(no)]
            zs = within(within([get(zm, k, q, o) for o in range(no)], gs, st + 4, 1), gs, st + 5, 2)
            for o, z in enumerate(over_o(k, q, zs, st + 6, (1, 2))):
                put(zm, k, q, o, z)
        for o in range(no):
            for q, z in enumerate(over_q(k, o, [get(zm, k, q, o) for q in range(chips)], st + 8, (1, 2))):
                put(zm, k, q, o, z)

    @pl.loop(0, nk + 1)
    def _(k):
        @pl.when(k < nk)
        def _():
            own_a2(k).wait()
            for r in range(1, chips):
                a2(k, r).wait_recv()
            d1(k).start()

        @pl.when(k == nk)
        def _():
            for j in range(nk):
                own_p2(j).start()
                for r in range(1, chips):
                    p2(j, r).start()

        @pl.when(k > 0)
        def _():
            far_local(k - 1)

    @pl.loop(0, chips)
    def _(q):
        for o in range(no):
            zs = [get(zm, k, q, o) for k in range(nk)]
            gs = [gidx(k, q, o) for k in range(nk)]
            zs = radix4(masks, zs, [[wpair(9 + s, g) for g in gs] for s in range(2)], (2, 1))
            zs = [gelu(z.astype(F32)).astype(BF) for z in zs]
            zs = radix4(masks, zs, [[wpair(st + 2 + s, g) for g in gs] for s in range(2)], (1, 2))
            for k in range(nk):
                put(zm, k, q, o, zs[k])

    for k in range(nk):
        for r in range(1, chips):
            a1(k, r).wait_send()
            p1(k, r).wait_send()
            a2(k, r).wait_send()

    @pl.loop(0, nk + 1)
    def _(k):
        @pl.when(k < nk)
        def _():
            near_local(k)
            d2(k).start()

        @pl.when(k > 0)
        def _():
            j = k - 1
            d2(j).wait_recv()
            for o in range(no):
                for q in range(chips):
                    put(t1, j, q, o, own_tile(masks, get(zm, j, q, o), get(zs2, j, q, o), wpair(st + 10, gidx(j, q, o))).astype(BF))
            own_a3(j).start()
            for r in range(1, chips):
                a3(j, r).start()

    @pl.loop(0, nk)
    def _(k):
        own_a3(k).wait()
        own_p2(k).wait()
        for r in range(1, chips):
            p2(k, r).wait_recv()
            a3(k, r).wait_recv()
        t_stage(t2, 1, k, (1, 2))
        own_a4(k).start()
        for r in range(1, chips):
            a4(k, r).start()

    @pl.loop(0, nk)
    def _(k):
        own_a4(k).wait()
        d1(k).wait_send()
        d2(k).wait_send()
        for r in range(1, chips):
            a4(k, r).wait_recv()
            p2(k, r).wait_send()
            a3(k, r).wait_send()
            a4(k, r).wait_send()


def solution(mesh):
    chips = mesh.shape["sp"] // 2

    def device_program(signal, w_first, w_second):
        rows, cols = signal.shape
        st, nb, two, br, _ = w_first.shape
        fold = LANES // br
        nk = 4
        no = nb // (chips * nk * fold)
        signal = signal.reshape(chips, no * fold, nk, br, cols)
        w1 = w_first.transpose(0, 2, 3, 4, 1)
        w2 = w_second.transpose(0, 2, 3, 4, 1)
        buf = pltpu.VMEM((nk, chips, no * fold, br, cols), BF)
        ns = nk * (chips - 1)
        pairs = [ns, ns, ns, ns, nk, nk, ns, ns]
        sems = [pltpu.SemaphoreType.DMA((n,)) for n in pairs for _ in range(2)]
        hbm = pl.BlockSpec(memory_space=pl.ANY)
        res = pl.pallas_call(
            functools.partial(kernel, chips),
            out_shape=jax.ShapeDtypeStruct(signal.shape, BF),
            in_specs=[hbm] * 3,
            out_specs=hbm,
            scratch_shapes=[
                buf, buf, buf, buf, buf, buf,
                pltpu.VMEM((2 * st, nb // fold, two, br, LANES), BF),
                pltpu.VMEM((2, nk, chips, 2, no, two, br, LANES), BF),
                pltpu.VMEM((2, two, br, br, nb), BF),
                pltpu.VMEM((br, nb // fold, two * LANES), BF),
                pltpu.VMEM((nb, nb), BF),
                pltpu.VMEM((nb // fold, nb), BF),
                *sems,
                pltpu.SemaphoreType.DMA((3 * nk,)),
                pltpu.SemaphoreType.DMA((2,)),
                pltpu.SemaphoreType.DMA((3 * nk,)),
            ],
            compiler_params=pltpu.CompilerParams(
                collective_id=0, has_side_effects=True, vmem_limit_bytes=60 * 2**20
            ),
        )(signal, w1, w2)
        return res.reshape(rows, cols)

    row_spec = P(("dp", "sp"), None)
    weight_spec = P(None, "sp", None, None, None)
    return jax.shard_map(device_program, mesh=mesh, in_specs=(row_spec, weight_spec, weight_spec), out_specs=row_spec, check_vma=False)
```

time: 264 us -> 246 us (0.932)
  Pallas kernels: 259 us -> 240 us
    pallas_call x1, Pallas kernels: 259 us -> 240 us  [device_program(): pl.pallas_call(functools.partial(kernel, chips), out_shape=jax.ShapeDtype...]
where the time goes in v3:
time: 246 us; the launch traced here: 244 us
  Pallas kernels  240 us (98%)
  local copies, waits for them, and re-layouts  4.47 us (2%)
    pallas_call x1, Pallas kernels, device_program(): pl.pallas_call(functools.partial(kernel, chips), out_shape=jax.ShapeDtype...  240 us

profile of v3, /device:TPU:81, one launch (start us, length us, event | category | flops | bytes accessed | tf_op | source)
XLA Modules:
  0.0 244.4 jit_solution(2868602641035892720)
XLA Ops:
  0.0 240.0 %shard_map.37 = bf16[4,16,4,32,256]{4,3,2,1,0:T(8,128)(2,1)} custom-call(bf16[4,16,4,32,256]{4,3,2,1,0:T(8,128)(2,1)} %bitcast.7, bf16[11,2,32,32,256]{4,3,2,1,0:T(8,128)(2,1)} %bitcast.5, bf16[11,2,32,32,256]{4,3,2,1,0:T(8,128)(2,1)} %bitcast.6), custom_call_target="tpu_custom_call" | custom-call | tf_op jit(solution)/shard_map/pallas_call | solution.py:387
  240.0 4.5 %copy.5 = bf16[8192,256]{1,0:T(8,128)(2,1)} copy(bf16[8192,256]{1,0:T(8,128)(2,1)} %bitcast.4) | data formatting | bytes 8388608

commit v4 on v3

--- a/solution.py
+++ b/solution.py
@@ -90,12 +90,15 @@
 
 def kernel(chips, sig, w1, w2, out,
            t1, z2, zs1, zm, zs2, t2, wl, wt, raw, mid, perm, sel,
-           a1s, a1r, p1s, p1r, a2s, a2r, p2s, p2r, d1s, d1r, d2s, d2r, a3s, a3r, a4s, a4r,
+           a1s, a1r, p1s, p1r, a2s, a2r, p2s, p2r, d1s, d1r, d2s, d2r, a3s, a3r, a4s, a4r, f1s, f1r, f2s, f2r,
            lsem, wsem, osem):
     d = lax.axis_index("sp")
     x = d // 2
     c = d % 2
     sib = x * 2 + (1 - c)
+    group = lax.axis_index("dp")
+    side = group % 2
+    mate = group + 1 - 2 * side
     br = wl.shape[3]
     fold = LANES // br
     nk = z2.shape[0]
@@ -111,6 +114,7 @@
     for r in range(1, chips):
         pl.semaphore_signal(barrier, inc=1, device_id=dev(peer(r)), device_id_type=MESH)
     pl.semaphore_signal(barrier, inc=1, device_id={"sp": sib}, device_id_type=MESH)
+    pl.semaphore_signal(barrier, inc=1, device_id={"dp": mate}, device_id_type=MESH)
 
     st = w1.shape[0]
 
@@ -159,7 +163,7 @@
     col = lax.broadcasted_iota(jnp.int32, sel.shape, 1)
     span = no * fold * nk
     sel[...] = (row == (col // span * nk + col % nk) * no + col // (fold * nk) % no).astype(F32).astype(BF)
-    pl.semaphore_wait(barrier, chips)
+    pl.semaphore_wait(barrier, chips + 1)
 
     def slot(k, r):
         return k * (chips - 1) + (r - 1)
@@ -170,15 +174,31 @@
     def a1(k, r):
         return remote(sig.at[peer(r), :, k], t1.at[k, x], a1s, a1r, slot(k, r), peer(r))
 
-    def p1(k, r):
-        return remote(wl.at[pl.ds(0, 2), wt_rows(peer(r), k)], wt.at[0, k, x], p1s, p1r, slot(k, r), peer(r))
+    def cross(m, i, r):
+        k = 2 * i + side
+        return remote(wl.at[pl.ds(m * st, 2), wt_rows(peer(r), k)], wt.at[m, k, x], (p1s, p2s)[m], (p1r, p2r)[m], slot(i, r), peer(r))
+
+    def share(m, i, r):
+        k = 2 * i + side
+        ref = wt.at[m, k, peer(r)]
+        return pltpu.make_async_remote_copy(
+            ref, ref, (f1s, f2s)[m].at[slot(i, r)], (f1r, f2r)[m].at[slot(i, r)], device_id={"dp": mate}, device_id_type=MESH)
+
+    def forward(m, i):
+        for r in range(1, chips):
+            cross(m, i, r).wait_recv()
+        for r in range(1, chips):
+            share(m, i, r).start()
+
+    def wait_shared(m, k):
+        @pl.when(k % 2 != side)
+        def _():
+            for r in range(1, chips):
+                share(m, k // 2, r).wait_recv()
 
     def a2(k, r):
         return remote(t1.at[k, peer(r)], z2.at[k, x], a2s, a2r, slot(k, r), peer(r))
 
-    def p2(k, r):
-        return remote(wl.at[pl.ds(st, 2), wt_rows(peer(r), k)], wt.at[1, k, x], p2s, p2r, slot(k, r), peer(r))
-
     def a3(k, r):
         return remote(t1.at[k, peer(r)], t2.at[k, x], a3s, a3r, slot(k, r), peer(r))
 
@@ -203,20 +223,17 @@
     def send_a1(k):
         for r in range(1, chips):
             a1(k, r).start()
-
-    def send_p1(k):
-        own_p1(k).start()
-        for r in range(1, chips):
-            p1(k, r).start()
 
     send_a1(0)
     send_a1(1)
     jobs(0, 2)
-    send_p1(0)
-    send_p1(1)
+    for i in range(nk // 2):
+        for r in range(1, chips):
+            cross(0, i, r).start()
     for k in range(2, nk):
         send_a1(k)
-        send_p1(k)
+    for k in range(nk):
+        own_p1(k).start()
 
     def get(buf, k, q, o):
         return buf[k, q, o * fold:(o + 1) * fold].reshape(fold * br, buf.shape[4])
@@ -236,20 +253,25 @@
             for p in range(chips):
                 put(buf, k, p, o, zs[p])
 
+    @pl.loop(0, nk // 2)
+    def _(i):
+        jobs(2 + 6 * i, 8 + 3 * i)
+        forward(0, i)
+
     @pl.loop(0, nk)
     def _(k):
-        jobs(2 + 4 * k, 6 + 4 * k)
+        jobs(11 + 2 * k, 13 + 2 * k)
         own_a1(k).wait()
         own_p1(k).wait()
-        for r in range(1, chips):
-            p1(k, r).wait_recv()
+        wait_shared(0, k)
+        for r in range(1, chips):
             a1(k, r).wait_recv()
         t_stage(t1, 0, k, (2, 1))
         own_a2(k).start()
         for r in range(1, chips):
             a2(k, r).start()
 
-    jobs(2 + 4 * nk, 2 * st)
+    jobs(11 + 2 * nk, 2 * st)
 
     def wpair(i, g):
         return wl[i, g, 0], wl[i, g, 1]
@@ -299,10 +321,11 @@
 
         @pl.when(k == nk)
         def _():
+            for i in range(nk // 2):
+                for r in range(1, chips):
+                    cross(1, i, r).start()
             for j in range(nk):
                 own_p2(j).start()
-                for r in range(1, chips):
-                    p2(j, r).start()
 
         @pl.when(k > 0)
         def _():
@@ -319,10 +342,13 @@
             for k in range(nk):
                 put(zm, k, q, o, zs[k])
 
+    @pl.loop(0, nk // 2)
+    def _(i):
+        forward(1, i)
+
     for k in range(nk):
         for r in range(1, chips):
             a1(k, r).wait_send()
-            p1(k, r).wait_send()
             a2(k, r).wait_send()
 
     @pl.loop(0, nk + 1)
@@ -347,8 +373,8 @@
     def _(k):
         own_a3(k).wait()
         own_p2(k).wait()
-        for r in range(1, chips):
-            p2(k, r).wait_recv()
+        wait_shared(1, k)
+        for r in range(1, chips):
             a3(k, r).wait_recv()
         t_stage(t2, 1, k, (1, 2))
         own_a4(k).start()
@@ -362,9 +388,15 @@
         d2(k).wait_send()
         for r in range(1, chips):
             a4(k, r).wait_recv()
-            p2(k, r).wait_send()
             a3(k, r).wait_send()
             a4(k, r).wait_send()
+
+    @pl.loop(0, nk // 2)
+    def _(i):
+        for m in range(2):
+            for r in range(1, chips):
+                cross(m, i, r).wait_send()
+                share(m, i, r).wait_send()
 
 
 def solution(mesh):
@@ -381,7 +413,7 @@
         w2 = w_second.transpose(0, 2, 3, 4, 1)
         buf = pltpu.VMEM((nk, chips, no * fold, br, cols), BF)
         ns = nk * (chips - 1)
-        pairs = [ns, ns, ns, ns, nk, nk, ns, ns]
+        pairs = [ns, ns // 2, ns, ns // 2, nk, nk, ns, ns, ns // 2, ns // 2]
         sems = [pltpu.SemaphoreType.DMA((n,)) for n in pairs for _ in range(2)]
         hbm = pl.BlockSpec(memory_space=pl.ANY)
         res = pl.pallas_call(

time: 246 us -> 235 us (0.955)
  Pallas kernels: 240 us -> 229 us
    pallas_call x1, Pallas kernels: 240 us -> 229 us  [device_program(): pl.pallas_call(functools.partial(kernel, chips), out_shape=jax.ShapeDtype...]
where the time goes in v4:
time: 235 us; the launch traced here: 234 us
  Pallas kernels  229 us (97%)
  local copies, waits for them, and re-layouts  4.47 us (2%)
    pallas_call x1, Pallas kernels, device_program(): pl.pallas_call(functools.partial(kernel, chips), out_shape=jax.ShapeDtype...  229 us

profile of v4, /device:TPU:81, one launch (start us, length us, event | category | flops | bytes accessed | tf_op | source)
XLA Modules:
  0.0 233.9 jit_solution(6370012826427784921)
XLA Ops:
  0.0 229.4 %shard_map.37 = bf16[4,16,4,32,256]{4,3,2,1,0:T(8,128)(2,1)} custom-call(bf16[4,16,4,32,256]{4,3,2,1,0:T(8,128)(2,1)} %bitcast.7, bf16[11,2,32,32,256]{4,3,2,1,0:T(8,128)(2,1)} %bitcast.5, bf16[11,2,32,32,256]{4,3,2,1,0:T(8,128)(2,1)} %bitcast.6), custom_call_target="tpu_custom_call" | custom-call | tf_op jit(solution)/shard_map/pallas_call | solution.py:419
  229.5 4.5 %copy.5 = bf16[8192,256]{1,0:T(8,128)(2,1)} copy(bf16[8192,256]{1,0:T(8,128)(2,1)} %bitcast.4) | data formatting | bytes 8388608

commit v5 on v4

--- a/solution.py
+++ b/solution.py
@@ -41,19 +41,6 @@
 def swap_rows(z, dist, br):
     n = z.shape[0] // br
     return jnp.concatenate([z[(k ^ dist) * br:((k ^ dist) + 1) * br] for k in range(n)], axis=0)
-
-
-def radix4(masks, zs, ws, order):
-    zs = list(zs)
-    for stage, dist in enumerate(order):
-        new = [None] * 4
-        for a in range(4):
-            b = a ^ dist
-            if a < b:
-                oa, ob = pair_tile(masks, zs[a], zs[b], ws[stage][a], ws[stage][b])
-                new[a], new[b] = oa.astype(BF), ob.astype(BF)
-        zs = new
-    return zs
 
 
 def gelu(x):
@@ -246,12 +233,22 @@
     def gidx(k, q, o):
         return (q * nk + k) * no + o
 
+    def pair_layer(buf, lines, dist, weight, post=None):
+        for line in lines:
+            for a in range(len(line)):
+                b = a ^ dist
+                if a < b:
+                    ka, kb = line[a], line[b]
+                    za, zb = pair_tile(masks, get(buf, *ka), get(buf, *kb), weight(*ka), weight(*kb))
+                    if post is not None:
+                        za, zb = post(za), post(zb)
+                    put(buf, *ka, za.astype(BF))
+                    put(buf, *kb, zb.astype(BF))
+
     def t_stage(buf, m, k, order):
-        for o in range(no):
-            ws = [[(wt[m, k, p, s, o, 0], wt[m, k, p, s, o, 1]) for p in range(chips)] for s in range(2)]
-            zs = radix4(masks, [get(buf, k, p, o) for p in range(chips)], ws, order)
-            for p in range(chips):
-                put(buf, k, p, o, zs[p])
+        lines = [[(k, p, o) for p in range(chips)] for o in range(no)]
+        for s, dist in enumerate(order):
+            pair_layer(buf, lines, dist, lambda k, p, o: (wt[m, k, p, s, o, 0], wt[m, k, p, s, o, 1]))
 
     @pl.loop(0, nk // 2)
     def _(i):
@@ -276,39 +273,41 @@
     def wpair(i, g):
         return wl[i, g, 0], wl[i, g, 1]
 
-    def within(zs, gs, i, dist):
-        return [own_tile(masks, z, swap_rows(z, dist, br), wpair(i, g)).astype(BF) for z, g in zip(zs, gs)]
-
-    def over_q(k, o, zs, first, order):
-        ws = [[wpair(first + s, gidx(k, q, o)) for q in range(chips)] for s in range(2)]
-        return radix4(masks, zs, ws, order)
-
-    def over_o(k, q, zs, first, order):
-        ws = [[wpair(first + s, gidx(k, q, o)) for o in range(no)] for s in range(2)]
-        return radix4(masks, zs, ws, order)
+    def local(i):
+        return lambda k, q, o: wpair(i, gidx(k, q, o))
+
+    def within(places, i, dist):
+        for key in places:
+            z = get(zm, *key)
+            put(zm, *key, own_tile(masks, z, swap_rows(z, dist, br), local(i)(*key)).astype(BF))
+
+    def over_q(k):
+        return [[(k, q, o) for q in range(chips)] for o in range(no)]
+
+    def over_o(k):
+        return [[(k, q, o) for o in range(no)] for q in range(chips)]
+
+    def places(k):
+        return [(k, q, o) for q in range(chips) for o in range(no)]
 
     def far_local(k):
         d1(k).wait_recv()
-        for o in range(no):
-            zs = [own_tile(masks, get(z2, k, q, o), get(zs1, k, q, o), wpair(2, gidx(k, q, o))).astype(BF) for q in range(chips)]
-            for q, z in enumerate(over_q(k, o, zs, 3, (2, 1))):
-                put(zm, k, q, o, z)
-        for q in range(chips):
-            gs = [gidx(k, q, o) for o in range(no)]
-            zs = over_o(k, q, [get(zm, k, q, o) for o in range(no)], 5, (2, 1))
-            zs = within(within(zs, gs, 7, 2), gs, 8, 1)
-            for o in range(no):
-                put(zm, k, q, o, zs[o])
+        for key in places(k):
+            put(zm, *key, own_tile(masks, get(z2, *key), get(zs1, *key), local(2)(*key)).astype(BF))
+        pair_layer(zm, over_q(k), 2, local(3))
+        pair_layer(zm, over_q(k), 1, local(4))
+        pair_layer(zm, over_o(k), 2, local(5))
+        pair_layer(zm, over_o(k), 1, local(6))
+        within(places(k), 7, 2)
+        within(places(k), 8, 1)
 
     def near_local(k):
-        for q in range(chips):
-            gs = [gidx(k, q, o) for o in range(no)]
-            zs = within(within([get(zm, k, q, o) for o in range(no)], gs, st + 4, 1), gs, st + 5, 2)
-            for o, z in enumerate(over_o(k, q, zs, st + 6, (1, 2))):
-                put(zm, k, q, o, z)
-        for o in range(no):
-            for q, z in enumerate(over_q(k, o, [get(zm, k, q, o) for q in range(chips)], st + 8, (1, 2))):
-                put(zm, k, q, o, z)
+        within(places(k), st + 4, 1)
+        within(places(k), st + 5, 2)
+        pair_layer(zm, over_o(k), 1, local(st + 6))
+        pair_layer(zm, over_o(k), 2, local(st + 7))
+        pair_layer(zm, over_q(k), 1, local(st + 8))
+        pair_layer(zm, over_q(k), 2, local(st + 9))
 
     @pl.loop(0, nk + 1)
     def _(k):
@@ -333,14 +332,11 @@
 
     @pl.loop(0, chips)
     def _(q):
-        for o in range(no):
-            zs = [get(zm, k, q, o) for k in range(nk)]
-            gs = [gidx(k, q, o) for k in range(nk)]
-            zs = radix4(masks, zs, [[wpair(9 + s, g) for g in gs] for s in range(2)], (2, 1))
-            zs = [gelu(z.astype(F32)).astype(BF) for z in zs]
-            zs = radix4(masks, zs, [[wpair(st + 2 + s, g) for g in gs] for s in range(2)], (1, 2))
-            for k in range(nk):
-                put(zm, k, q, o, zs[k])
+        lines = [[(k, q, o) for k in range(nk)] for o in range(no)]
+        pair_layer(zm, lines, 2, local(9))
+        pair_layer(zm, lines, 1, local(10), lambda z: gelu(z.astype(BF).astype(F32)))
+        pair_layer(zm, lines, 1, local(st + 2))
+        pair_layer(zm, lines, 2, local(st + 3))
 
     @pl.loop(0, nk // 2)
     def _(i):
@@ -418,9 +414,9 @@
         hbm = pl.BlockSpec(memory_space=pl.ANY)
         res = pl.pallas_call(
             functools.partial(kernel, chips),
-            out_shape=jax.ShapeDtypeStruct(signal.shape, BF),
+            out_shape=pltpu.VMEM(signal.shape, BF),
             in_specs=[hbm] * 3,
-            out_specs=hbm,
+            out_specs=pl.BlockSpec(memory_space=pltpu.VMEM),
             scratch_shapes=[
                 buf, buf, buf, buf, buf, buf,
                 pltpu.VMEM((2 * st, nb // fold, two, br, LANES), BF),
@@ -435,7 +431,7 @@
                 pltpu.SemaphoreType.DMA((3 * nk,)),
             ],
             compiler_params=pltpu.CompilerParams(
-                collective_id=0, has_side_effects=True, vmem_limit_bytes=60 * 2**20
+                collective_id=0, has_side_effects=True, vmem_limit_bytes=56 * 2**20
             ),
         )(signal, w1, w2)
         return res.reshape(rows, cols)

time: 235 us -> 225 us (0.957)
  Pallas kernels: 229 us -> 223 us
  local copies, waits for them, and re-layouts: 4.47 us -> 2.02 us
    pallas_call x1, Pallas kernels: 229 us -> 223 us  [device_program(): pl.pallas_call(functools.partial(kernel, chips), out_shape=pltpu.VMEM(sig...]
    unnamed x1, local copies, waits for them, and re-layouts: 4.47 us -> 2.02 us
where the time goes in v5:
time: 225 us
  Pallas kernels  223 us (99%)
    pallas_call x1, Pallas kernels, device_program(): pl.pallas_call(functools.partial(kernel, chips), out_shape=pltpu.VMEM(sig...  223 us

profile of v5, /device:TPU:81, one launch (start us, length us, event | category | flops | bytes accessed | tf_op | source)
XLA Modules:
  0.0 225.2 jit_solution(13928746280872816158)
XLA Ops:
  0.0 223.2 %shard_map.37 = bf16[4,16,4,32,256]{4,3,2,1,0:T(8,128)(2,1)S(1)} custom-call(bf16[4,16,4,32,256]{4,3,2,1,0:T(8,128)(2,1)} %bitcast.7, bf16[11,2,32,32,256]{4,3,2,1,0:T(8,128)(2,1)} %bitcast.5, bf16[11,2,32,32,256]{4,3,2,1,0:T(8,128)(2,1)} %bitcast.6), custom_call_target="tpu_custom_call" | custom-call | tf_op jit(solution)/shard_map/pallas_call | solution.py:415
  223.2 2.0 copy.5

commit v6 on v5

--- a/solution.py
+++ b/solution.py
@@ -75,7 +75,7 @@
                         dst[g0 + g, t, half * 16:(half + 1) * 16, :] = res[g * 16:(g + 1) * 16, t * LANES:(t + 1) * LANES]
 
 
-def kernel(chips, sig, w1, w2, out,
+def kernel(chips, ways, sig, w1, w2, out,
            t1, z2, zs1, zm, zs2, t2, wl, wt, raw, mid, perm, sel,
            a1s, a1r, p1s, p1r, a2s, a2r, p2s, p2r, d1s, d1r, d2s, d2r, a3s, a3r, a4s, a4r, f1s, f1r, f2s, f2r,
            lsem, wsem, osem):
@@ -84,8 +84,11 @@
     c = d % 2
     sib = x * 2 + (1 - c)
     group = lax.axis_index("dp")
-    side = group % 2
-    mate = group + 1 - 2 * side
+    side = group % ways
+
+    def mate(j):
+        return {"dp": group - side + (side + j) % ways}
+
     br = wl.shape[3]
     fold = LANES // br
     nk = z2.shape[0]
@@ -101,7 +104,8 @@
     for r in range(1, chips):
         pl.semaphore_signal(barrier, inc=1, device_id=dev(peer(r)), device_id_type=MESH)
     pl.semaphore_signal(barrier, inc=1, device_id={"sp": sib}, device_id_type=MESH)
-    pl.semaphore_signal(barrier, inc=1, device_id={"dp": mate}, device_id_type=MESH)
+    for j in range(1, ways):
+        pl.semaphore_signal(barrier, inc=1, device_id=mate(j), device_id_type=MESH)
 
     st = w1.shape[0]
 
@@ -150,7 +154,7 @@
     col = lax.broadcasted_iota(jnp.int32, sel.shape, 1)
     span = no * fold * nk
     sel[...] = (row == (col // span * nk + col % nk) * no + col // (fold * nk) % no).astype(F32).astype(BF)
-    pl.semaphore_wait(barrier, chips + 1)
+    pl.semaphore_wait(barrier, chips + ways - 1)
 
     def slot(k, r):
         return k * (chips - 1) + (r - 1)
@@ -161,27 +165,27 @@
     def a1(k, r):
         return remote(sig.at[peer(r), :, k], t1.at[k, x], a1s, a1r, slot(k, r), peer(r))
 
-    def cross(m, i, r):
-        k = 2 * i + side
-        return remote(wl.at[pl.ds(m * st, 2), wt_rows(peer(r), k)], wt.at[m, k, x], (p1s, p2s)[m], (p1r, p2r)[m], slot(i, r), peer(r))
-
-    def share(m, i, r):
-        k = 2 * i + side
-        ref = wt.at[m, k, peer(r)]
+    def cross(m, r):
+        return remote(wl.at[pl.ds(m * st, 2), wt_rows(peer(r), side)], wt.at[m, side, x], (p1s, p2s)[m], (p1r, p2r)[m], r - 1, peer(r))
+
+    def share(m, j, r):
+        ref = wt.at[m, side, peer(r)]
+        i = (j - 1) * (chips - 1) + r - 1
         return pltpu.make_async_remote_copy(
-            ref, ref, (f1s, f2s)[m].at[slot(i, r)], (f1r, f2r)[m].at[slot(i, r)], device_id={"dp": mate}, device_id_type=MESH)
-
-    def forward(m, i):
-        for r in range(1, chips):
-            cross(m, i, r).wait_recv()
-        for r in range(1, chips):
-            share(m, i, r).start()
+            ref, ref, (f1s, f2s)[m].at[i], (f1r, f2r)[m].at[i], device_id=mate(j), device_id_type=MESH)
+
+    def forward(m):
+        for r in range(1, chips):
+            cross(m, r).wait_recv()
+        for j in range(1, ways):
+            for r in range(1, chips):
+                share(m, j, r).start()
 
     def wait_shared(m, k):
-        @pl.when(k % 2 != side)
+        @pl.when(k != side)
         def _():
             for r in range(1, chips):
-                share(m, k // 2, r).wait_recv()
+                share(m, (side - k + ways) % ways, r).wait_recv()
 
     def a2(k, r):
         return remote(t1.at[k, peer(r)], z2.at[k, x], a2s, a2r, slot(k, r), peer(r))
@@ -212,12 +216,10 @@
             a1(k, r).start()
 
     send_a1(0)
-    send_a1(1)
     jobs(0, 2)
-    for i in range(nk // 2):
-        for r in range(1, chips):
-            cross(0, i, r).start()
-    for k in range(2, nk):
+    for r in range(1, chips):
+        cross(0, r).start()
+    for k in range(1, nk):
         send_a1(k)
     for k in range(nk):
         own_p1(k).start()
@@ -250,14 +252,12 @@
         for s, dist in enumerate(order):
             pair_layer(buf, lines, dist, lambda k, p, o: (wt[m, k, p, s, o, 0], wt[m, k, p, s, o, 1]))
 
-    @pl.loop(0, nk // 2)
-    def _(i):
-        jobs(2 + 6 * i, 8 + 3 * i)
-        forward(0, i)
+    jobs(2, 6)
+    forward(0)
 
     @pl.loop(0, nk)
     def _(k):
-        jobs(11 + 2 * k, 13 + 2 * k)
+        jobs(6 + 3 * k, 9 + 3 * k)
         own_a1(k).wait()
         own_p1(k).wait()
         wait_shared(0, k)
@@ -268,7 +268,7 @@
         for r in range(1, chips):
             a2(k, r).start()
 
-    jobs(11 + 2 * nk, 2 * st)
+    jobs(6 + 3 * nk, 2 * st)
 
     def wpair(i, g):
         return wl[i, g, 0], wl[i, g, 1]
@@ -320,9 +320,8 @@
 
         @pl.when(k == nk)
         def _():
-            for i in range(nk // 2):
-                for r in range(1, chips):
-                    cross(1, i, r).start()
+            for r in range(1, chips):
+                cross(1, r).start()
             for j in range(nk):
                 own_p2(j).start()
 
@@ -338,9 +337,7 @@
         pair_layer(zm, lines, 1, local(st + 2))
         pair_layer(zm, lines, 2, local(st + 3))
 
-    @pl.loop(0, nk // 2)
-    def _(i):
-        forward(1, i)
+    forward(1)
 
     for k in range(nk):
         for r in range(1, chips):
@@ -387,12 +384,11 @@
             a3(k, r).wait_send()
             a4(k, r).wait_send()
 
-    @pl.loop(0, nk // 2)
-    def _(i):
-        for m in range(2):
-            for r in range(1, chips):
-                cross(m, i, r).wait_send()
-                share(m, i, r).wait_send()
+    for m in range(2):
+        for r in range(1, chips):
+            cross(m, r).wait_send()
+            for j in range(1, ways):
+                share(m, j, r).wait_send()
 
 
 def solution(mesh):
@@ -409,11 +405,12 @@
         w2 = w_second.transpose(0, 2, 3, 4, 1)
         buf = pltpu.VMEM((nk, chips, no * fold, br, cols), BF)
         ns = nk * (chips - 1)
-        pairs = [ns, ns // 2, ns, ns // 2, nk, nk, ns, ns, ns // 2, ns // 2]
+        fs = (nk - 1) * (chips - 1)
+        pairs = [ns, chips - 1, ns, chips - 1, nk, nk, ns, ns, fs, fs]
         sems = [pltpu.SemaphoreType.DMA((n,)) for n in pairs for _ in range(2)]
         hbm = pl.BlockSpec(memory_space=pl.ANY)
         res = pl.pallas_call(
-            functools.partial(kernel, chips),
+            functools.partial(kernel, chips, nk),
             out_shape=pltpu.VMEM(signal.shape, BF),
             in_specs=[hbm] * 3,
             out_specs=pl.BlockSpec(memory_space=pltpu.VMEM),

time: 225 us -> 217 us (0.964)
  Pallas kernels: 223 us -> 215 us
    pallas_call x1, Pallas kernels: 223 us -> 215 us  [device_program(): pl.pallas_call(functools.partial(kernel, chips, nk), out_shape=pltpu.VMEM...]
where the time goes in v6:
time: 217 us
  Pallas kernels  215 us (99%)
    pallas_call x1, Pallas kernels, device_program(): pl.pallas_call(functools.partial(kernel, chips, nk), out_shape=pltpu.VMEM...  215 us

profile of v6, /device:TPU:81, one launch (start us, length us, event | category | flops | bytes accessed | tf_op | source)
XLA Modules:
  0.0 217.0 jit_solution(7686838882851196441)
XLA Ops:
  0.0 215.0 %shard_map.37 = bf16[4,16,4,32,256]{4,3,2,1,0:T(8,128)(2,1)S(1)} custom-call(bf16[4,16,4,32,256]{4,3,2,1,0:T(8,128)(2,1)} %bitcast.7, bf16[11,2,32,32,256]{4,3,2,1,0:T(8,128)(2,1)} %bitcast.5, bf16[11,2,32,32,256]{4,3,2,1,0:T(8,128)(2,1)} %bitcast.6), custom_call_target="tpu_custom_call" | custom-call | tf_op jit(solution)/shard_map/pallas_call | solution.py:412
  215.0 2.0 copy.5

commit v7 on v6

--- a/solution.py
+++ b/solution.py
@@ -91,8 +91,9 @@
 
     br = wl.shape[3]
     fold = LANES // br
-    nk = z2.shape[0]
-    no = z2.shape[2] // fold
+    halves, nk = z2.shape[:2]
+    width = z2.shape[5]
+    no = z2.shape[3] // fold
 
     def peer(r):
         return (x + r) % chips
@@ -187,29 +188,39 @@
             for r in range(1, chips):
                 share(m, (side - k + ways) % ways, r).wait_recv()
 
-    def a2(k, r):
-        return remote(t1.at[k, peer(r)], z2.at[k, x], a2s, a2r, slot(k, r), peer(r))
-
-    def a3(k, r):
-        return remote(t1.at[k, peer(r)], t2.at[k, x], a3s, a3r, slot(k, r), peer(r))
+    def lanes(h):
+        return pl.ds(pl.multiple_of(h * width, width), width)
+
+    def half_slot(h, k, r):
+        return slot(h * nk + k, r)
+
+    def a2(h, k, r):
+        return remote(t1.at[k, peer(r), :, :, lanes(h)], z2.at[h, k, x], a2s, a2r, half_slot(h, k, r), peer(r))
+
+    def a3(h, k, r):
+        return remote(z2.at[h, k, peer(r)], t2.at[k, x, :, :, lanes(h)], a3s, a3r, half_slot(h, k, r), peer(r))
 
     def a4(k, r):
         return remote(t2.at[k, peer(r)], out.at[x, :, k], a4s, a4r, slot(k, r), peer(r))
 
-    def d1(k):
-        return pltpu.make_async_remote_copy(z2.at[k], zs1.at[k], d1s.at[k], d1r.at[k], device_id={"sp": sib}, device_id_type=MESH)
-
-    def d2(k):
-        return pltpu.make_async_remote_copy(zm.at[k], zs2.at[k], d2s.at[k], d2r.at[k], device_id={"sp": sib}, device_id_type=MESH)
-
-    def own_a2(k):
-        return pltpu.make_async_copy(t1.at[k, x], z2.at[k, x], osem.at[k])
-
-    def own_a3(k):
-        return pltpu.make_async_copy(t1.at[k, x], t2.at[k, x], osem.at[nk + k])
+    def sibling(src, dst, ss, rs, h, k):
+        return pltpu.make_async_remote_copy(
+            src.at[h, k], dst.at[h, k], ss.at[h * nk + k], rs.at[h * nk + k], device_id={"sp": sib}, device_id_type=MESH)
+
+    def d1(h, k):
+        return sibling(z2, zs1, d1s, d1r, h, k)
+
+    def d2(h, k):
+        return sibling(zm, zs2, d2s, d2r, h, k)
+
+    def own_a2(h, k):
+        return pltpu.make_async_copy(t1.at[k, x, :, :, lanes(h)], z2.at[h, k, x], osem.at[h * nk + k])
+
+    def own_a3(h, k):
+        return pltpu.make_async_copy(z2.at[h, k, x], t2.at[k, x, :, :, lanes(h)], osem.at[(halves + h) * nk + k])
 
     def own_a4(k):
-        return pltpu.make_async_copy(t2.at[k, x], out.at[x, :, k], osem.at[2 * nk + k])
+        return pltpu.make_async_copy(t2.at[k, x], out.at[x, :, k], osem.at[2 * halves * nk + k])
 
     def send_a1(k):
         for r in range(1, chips):
@@ -255,6 +266,11 @@
     jobs(2, 6)
     forward(0)
 
+    def send_a2(h, k):
+        own_a2(h, k).start()
+        for r in range(1, chips):
+            a2(h, k, r).start()
+
     @pl.loop(0, nk)
     def _(k):
         jobs(6 + 3 * k, 9 + 3 * k)
@@ -264,9 +280,12 @@
         for r in range(1, chips):
             a1(k, r).wait_recv()
         t_stage(t1, 0, k, (2, 1))
-        own_a2(k).start()
-        for r in range(1, chips):
-            a2(k, r).start()
+        send_a2(0, k)
+
+    @pl.loop(1, halves)
+    def _(h):
+        for k in range(nk):
+            send_a2(h, k)
 
     jobs(6 + 3 * nk, 2 * st)
 
@@ -276,10 +295,10 @@
     def local(i):
         return lambda k, q, o: wpair(i, gidx(k, q, o))
 
-    def within(places, i, dist):
+    def within(buf, places, i, dist):
         for key in places:
-            z = get(zm, *key)
-            put(zm, *key, own_tile(masks, z, swap_rows(z, dist, br), local(i)(*key)).astype(BF))
+            z = get(buf, *key)
+            put(buf, *key, own_tile(masks, z, swap_rows(z, dist, br), local(i)(*key)).astype(BF))
 
     def over_q(k):
         return [[(k, q, o) for q in range(chips)] for o in range(no)]
@@ -290,85 +309,86 @@
     def places(k):
         return [(k, q, o) for q in range(chips) for o in range(no)]
 
-    def far_local(k):
-        d1(k).wait_recv()
+    def far_local(h, k):
+        d1(h, k).wait_recv()
+        buf = zm.at[h]
         for key in places(k):
-            put(zm, *key, own_tile(masks, get(z2, *key), get(zs1, *key), local(2)(*key)).astype(BF))
-        pair_layer(zm, over_q(k), 2, local(3))
-        pair_layer(zm, over_q(k), 1, local(4))
-        pair_layer(zm, over_o(k), 2, local(5))
-        pair_layer(zm, over_o(k), 1, local(6))
-        within(places(k), 7, 2)
-        within(places(k), 8, 1)
-
-    def near_local(k):
-        within(places(k), st + 4, 1)
-        within(places(k), st + 5, 2)
-        pair_layer(zm, over_o(k), 1, local(st + 6))
-        pair_layer(zm, over_o(k), 2, local(st + 7))
-        pair_layer(zm, over_q(k), 1, local(st + 8))
-        pair_layer(zm, over_q(k), 2, local(st + 9))
-
-    @pl.loop(0, nk + 1)
-    def _(k):
-        @pl.when(k < nk)
-        def _():
-            own_a2(k).wait()
-            for r in range(1, chips):
-                a2(k, r).wait_recv()
-            d1(k).start()
-
-        @pl.when(k == nk)
+            put(buf, *key, own_tile(masks, get(z2.at[h], *key), get(zs1.at[h], *key), local(2)(*key)).astype(BF))
+        pair_layer(buf, over_q(k), 2, local(3))
+        pair_layer(buf, over_q(k), 1, local(4))
+        pair_layer(buf, over_o(k), 2, local(5))
+        pair_layer(buf, over_o(k), 1, local(6))
+        within(buf, places(k), 7, 2)
+        within(buf, places(k), 8, 1)
+
+    def near_local(h, k):
+        buf = zm.at[h]
+        within(buf, places(k), st + 4, 1)
+        within(buf, places(k), st + 5, 2)
+        pair_layer(buf, over_o(k), 1, local(st + 6))
+        pair_layer(buf, over_o(k), 2, local(st + 7))
+        pair_layer(buf, over_q(k), 1, local(st + 8))
+        pair_layer(buf, over_q(k), 2, local(st + 9))
+
+    @pl.loop(0, halves)
+    def _(h):
+        @pl.loop(0, nk + 1)
+        def _(k):
+            @pl.when(k < nk)
+            def _():
+                own_a2(h, k).wait()
+                for r in range(1, chips):
+                    a2(h, k, r).wait_recv()
+                d1(h, k).start()
+
+            @pl.when(k > 0)
+            def _():
+                far_local(h, k - 1)
+
+        @pl.when(h == halves - 1)
         def _():
             for r in range(1, chips):
                 cross(1, r).start()
             for j in range(nk):
                 own_p2(j).start()
 
-        @pl.when(k > 0)
-        def _():
-            far_local(k - 1)
-
-    @pl.loop(0, chips)
-    def _(q):
-        lines = [[(k, q, o) for k in range(nk)] for o in range(no)]
-        pair_layer(zm, lines, 2, local(9))
-        pair_layer(zm, lines, 1, local(10), lambda z: gelu(z.astype(BF).astype(F32)))
-        pair_layer(zm, lines, 1, local(st + 2))
-        pair_layer(zm, lines, 2, local(st + 3))
+        @pl.loop(0, chips)
+        def _(q):
+            lines = [[(k, q, o) for k in range(nk)] for o in range(no)]
+            buf = zm.at[h]
+            pair_layer(buf, lines, 2, local(9))
+            pair_layer(buf, lines, 1, local(10), lambda z: gelu(z.astype(BF).astype(F32)))
+            pair_layer(buf, lines, 1, local(st + 2))
+            pair_layer(buf, lines, 2, local(st + 3))
+
+        @pl.loop(0, nk + 1)
+        def _(k):
+            @pl.when(k < nk)
+            def _():
+                near_local(h, k)
+                d2(h, k).start()
+
+            @pl.when(k > 0)
+            def _():
+                j = k - 1
+                d1(h, j).wait_send()
+                d2(h, j).wait_recv()
+                for key in places(j):
+                    put(z2.at[h], *key, own_tile(masks, get(zm.at[h], *key), get(zs2.at[h], *key), local(st + 10)(*key)).astype(BF))
+                own_a3(h, j).start()
+                for r in range(1, chips):
+                    a3(h, j, r).start()
 
     forward(1)
-
-    for k in range(nk):
-        for r in range(1, chips):
-            a1(k, r).wait_send()
-            a2(k, r).wait_send()
-
-    @pl.loop(0, nk + 1)
-    def _(k):
-        @pl.when(k < nk)
-        def _():
-            near_local(k)
-            d2(k).start()
-
-        @pl.when(k > 0)
-        def _():
-            j = k - 1
-            d2(j).wait_recv()
-            for o in range(no):
-                for q in range(chips):
-                    put(t1, j, q, o, own_tile(masks, get(zm, j, q, o), get(zs2, j, q, o), wpair(st + 10, gidx(j, q, o))).astype(BF))
-            own_a3(j).start()
-            for r in range(1, chips):
-                a3(j, r).start()
 
     @pl.loop(0, nk)
     def _(k):
-        own_a3(k).wait()
         own_p2(k).wait()
         wait_shared(1, k)
-        for r in range(1, chips):
-            a3(k, r).wait_recv()
+        for h in range(halves):
+            own_a3(h, k).wait()
+            for r in range(1, chips):
+                a3(h, k, r).wait_recv()
         t_stage(t2, 1, k, (1, 2))
         own_a4(k).start()
         for r in range(1, chips):
@@ -377,12 +397,15 @@
     @pl.loop(0, nk)
     def _(k):
         own_a4(k).wait()
-        d1(k).wait_send()
-        d2(k).wait_send()
-        for r in range(1, chips):
+        for r in range(1, chips):
+            a1(k, r).wait_send()
             a4(k, r).wait_recv()
-            a3(k, r).wait_send()
             a4(k, r).wait_send()
+        for h in range(halves):
+            d2(h, k).wait_send()
+            for r in range(1, chips):
+                a2(h, k, r).wait_send()
+                a3(h, k, r).wait_send()
 
     for m in range(2):
         for r in range(1, chips):
@@ -404,9 +427,11 @@
         w1 = w_first.transpose(0, 2, 3, 4, 1)
         w2 = w_second.transpose(0, 2, 3, 4, 1)
         buf = pltpu.VMEM((nk, chips, no * fold, br, cols), BF)
+        half = pltpu.VMEM((cols // LANES, nk, chips, no * fold, br, LANES), BF)
         ns = nk * (chips - 1)
+        hs = cols // LANES
         fs = (nk - 1) * (chips - 1)
-        pairs = [ns, chips - 1, ns, chips - 1, nk, nk, ns, ns, fs, fs]
+        pairs = [ns, chips - 1, hs * ns, chips - 1, hs * nk, hs * nk, hs * ns, ns, fs, fs]
         sems = [pltpu.SemaphoreType.DMA((n,)) for n in pairs for _ in range(2)]
         hbm = pl.BlockSpec(memory_space=pl.ANY)
         res = pl.pallas_call(
@@ -415,7 +440,7 @@
             in_specs=[hbm] * 3,
             out_specs=pl.BlockSpec(memory_space=pltpu.VMEM),
             scratch_shapes=[
-                buf, buf, buf, buf, buf, buf,
+                buf, half, half, half, half, buf,
                 pltpu.VMEM((2 * st, nb // fold, two, br, LANES), BF),
                 pltpu.VMEM((2, nk, chips, 2, no, two, br, LANES), BF),
                 pltpu.VMEM((2, two, br, br, nb), BF),
@@ -425,7 +450,7 @@
                 *sems,
                 pltpu.SemaphoreType.DMA((3 * nk,)),
                 pltpu.SemaphoreType.DMA((2,)),
-                pltpu.SemaphoreType.DMA((3 * nk,)),
+                pltpu.SemaphoreType.DMA(((2 * hs + 1) * nk,)),
             ],
             compiler_params=pltpu.CompilerParams(
                 collective_id=0, has_side_effects=True, vmem_limit_bytes=56 * 2**20

time: 217 us -> 204 us (0.940)
  Pallas kernels: 215 us -> 201 us
    pallas_call x1, Pallas kernels: 215 us -> 201 us  [device_program(): pl.pallas_call(functools.partial(kernel, chips, nk), out_shape=pltpu.VMEM...]
where the time goes in v7:
time: 204 us; the launch traced here: 203 us
  Pallas kernels  201 us (99%)
    pallas_call x1, Pallas kernels, device_program(): pl.pallas_call(functools.partial(kernel, chips, nk), out_shape=pltpu.VMEM...  201 us

profile of v7, /device:TPU:81, one launch (start us, length us, event | category | flops | bytes accessed | tf_op | source)
XLA Modules:
  0.0 203.5 jit_solution(12794933299812883539)
XLA Ops:
  0.0 201.5 %shard_map.37 = bf16[4,16,4,32,256]{4,3,2,1,0:T(8,128)(2,1)S(1)} custom-call(bf16[4,16,4,32,256]{4,3,2,1,0:T(8,128)(2,1)} %bitcast.7, bf16[11,2,32,32,256]{4,3,2,1,0:T(8,128)(2,1)} %bitcast.5, bf16[11,2,32,32,256]{4,3,2,1,0:T(8,128)(2,1)} %bitcast.6), custom_call_target="tpu_custom_call" | custom-call | tf_op jit(solution)/shard_map/pallas_call | solution.py:437
  201.5 2.0 copy.5

commit v8 on v7

--- a/solution.py
+++ b/solution.py
@@ -147,6 +147,78 @@
     load_w(w1, 0, 0).start()
     for k in range(nk):
         own_a1(k).start()
+    pl.semaphore_wait(barrier, chips + ways - 1)
+
+    def slot(k, r):
+        return k * (chips - 1) + (r - 1)
+
+    def remote(src, dst, ss, rs, i, q):
+        return pltpu.make_async_remote_copy(src, dst, ss.at[i], rs.at[i], device_id=dev(q), device_id_type=MESH)
+
+    def a1(k, r):
+        return remote(sig.at[peer(r), :, k], t1.at[k, x], a1s, a1r, slot(k, r), peer(r))
+
+    def cross(m, r):
+        return remote(wl.at[pl.ds(m * st, 2), wt_rows(peer(r), side)], wt.at[m, side, x], (p1s, p2s)[m], (p1r, p2r)[m], r - 1, peer(r))
+
+    def share(m, j, r):
+        ref = wt.at[m, side, peer(r)]
+        i = (j - 1) * (chips - 1) + r - 1
+        return pltpu.make_async_remote_copy(
+            ref, ref, (f1s, f2s)[m].at[i], (f1r, f2r)[m].at[i], device_id=mate(j), device_id_type=MESH)
+
+    def forward(m):
+        for r in range(1, chips):
+            cross(m, r).wait_recv()
+        for j in range(1, ways):
+            for r in range(1, chips):
+                share(m, j, r).start()
+
+    def wait_shared(m, k):
+        @pl.when(k != side)
+        def _():
+            for r in range(1, chips):
+                share(m, (side - k + ways) % ways, r).wait_recv()
+
+    def lanes(h):
+        return pl.ds(pl.multiple_of(h * width, width), width)
+
+    def half_slot(h, k, r):
+        return slot(h * nk + k, r)
+
+    def a2(h, k, r):
+        return remote(t1.at[k, peer(r), :, :, lanes(h)], z2.at[h, k, x], a2s, a2r, half_slot(h, k, r), peer(r))
+
+    def a3(h, k, r):
+        return remote(z2.at[h, k, peer(r)], t2.at[k, x, :, :, lanes(h)], a3s, a3r, half_slot(h, k, r), peer(r))
+
+    def a4(k, r):
+        return remote(t2.at[k, peer(r)], out.at[x, :, k], a4s, a4r, slot(k, r), peer(r))
+
+    def sibling(src, dst, ss, rs, h, k):
+        return pltpu.make_async_remote_copy(
+            src.at[h, k], dst.at[h, k], ss.at[h * nk + k], rs.at[h * nk + k], device_id={"sp": sib}, device_id_type=MESH)
+
+    def d1(h, k):
+        return sibling(z2, zs1, d1s, d1r, h, k)
+
+    def d2(h, k):
+        return sibling(zm, zs2, d2s, d2r, h, k)
+
+    def own_a2(h, k):
+        return pltpu.make_async_copy(t1.at[k, x, :, :, lanes(h)], z2.at[h, k, x], osem.at[h * nk + k])
+
+    def own_a3(h, k):
+        return pltpu.make_async_copy(z2.at[h, k, x], t2.at[k, x, :, :, lanes(h)], osem.at[(halves + h) * nk + k])
+
+    def own_a4(k):
+        return pltpu.make_async_copy(t2.at[k, x], out.at[x, :, k], osem.at[2 * halves * nk + k])
+
+    def send_a1(k):
+        for r in range(1, chips):
+            a1(k, r).start()
+
+    send_a1(0)
     row = lax.broadcasted_iota(jnp.int32, perm.shape, 0)
     col = lax.broadcasted_iota(jnp.int32, perm.shape, 1)
     tile = perm.shape[0] // 16
@@ -155,78 +227,6 @@
     col = lax.broadcasted_iota(jnp.int32, sel.shape, 1)
     span = no * fold * nk
     sel[...] = (row == (col // span * nk + col % nk) * no + col // (fold * nk) % no).astype(F32).astype(BF)
-    pl.semaphore_wait(barrier, chips + ways - 1)
-
-    def slot(k, r):
-        return k * (chips - 1) + (r - 1)
-
-    def remote(src, dst, ss, rs, i, q):
-        return pltpu.make_async_remote_copy(src, dst, ss.at[i], rs.at[i], device_id=dev(q), device_id_type=MESH)
-
-    def a1(k, r):
-        return remote(sig.at[peer(r), :, k], t1.at[k, x], a1s, a1r, slot(k, r), peer(r))
-
-    def cross(m, r):
-        return remote(wl.at[pl.ds(m * st, 2), wt_rows(peer(r), side)], wt.at[m, side, x], (p1s, p2s)[m], (p1r, p2r)[m], r - 1, peer(r))
-
-    def share(m, j, r):
-        ref = wt.at[m, side, peer(r)]
-        i = (j - 1) * (chips - 1) + r - 1
-        return pltpu.make_async_remote_copy(
-            ref, ref, (f1s, f2s)[m].at[i], (f1r, f2r)[m].at[i], device_id=mate(j), device_id_type=MESH)
-
-    def forward(m):
-        for r in range(1, chips):
-            cross(m, r).wait_recv()
-        for j in range(1, ways):
-            for r in range(1, chips):
-                share(m, j, r).start()
-
-    def wait_shared(m, k):
-        @pl.when(k != side)
-        def _():
-            for r in range(1, chips):
-                share(m, (side - k + ways) % ways, r).wait_recv()
-
-    def lanes(h):
-        return pl.ds(pl.multiple_of(h * width, width), width)
-
-    def half_slot(h, k, r):
-        return slot(h * nk + k, r)
-
-    def a2(h, k, r):
-        return remote(t1.at[k, peer(r), :, :, lanes(h)], z2.at[h, k, x], a2s, a2r, half_slot(h, k, r), peer(r))
-
-    def a3(h, k, r):
-        return remote(z2.at[h, k, peer(r)], t2.at[k, x, :, :, lanes(h)], a3s, a3r, half_slot(h, k, r), peer(r))
-
-    def a4(k, r):
-        return remote(t2.at[k, peer(r)], out.at[x, :, k], a4s, a4r, slot(k, r), peer(r))
-
-    def sibling(src, dst, ss, rs, h, k):
-        return pltpu.make_async_remote_copy(
-            src.at[h, k], dst.at[h, k], ss.at[h * nk + k], rs.at[h * nk + k], device_id={"sp": sib}, device_id_type=MESH)
-
-    def d1(h, k):
-        return sibling(z2, zs1, d1s, d1r, h, k)
-
-    def d2(h, k):
-        return sibling(zm, zs2, d2s, d2r, h, k)
-
-    def own_a2(h, k):
-        return pltpu.make_async_copy(t1.at[k, x, :, :, lanes(h)], z2.at[h, k, x], osem.at[h * nk + k])
-
-    def own_a3(h, k):
-        return pltpu.make_async_copy(z2.at[h, k, x], t2.at[k, x, :, :, lanes(h)], osem.at[(halves + h) * nk + k])
-
-    def own_a4(k):
-        return pltpu.make_async_copy(t2.at[k, x], out.at[x, :, k], osem.at[2 * halves * nk + k])
-
-    def send_a1(k):
-        for r in range(1, chips):
-            a1(k, r).start()
-
-    send_a1(0)
     jobs(0, 2)
     for r in range(1, chips):
         cross(0, r).start()
@@ -282,6 +282,11 @@
         t_stage(t1, 0, k, (2, 1))
         send_a2(0, k)
 
+    for r in range(1, chips):
+        cross(1, r).start()
+    for k in range(nk):
+        own_p2(k).start()
+
     @pl.loop(1, halves)
     def _(h):
         for k in range(nk):
@@ -345,13 +350,6 @@
             def _():
                 far_local(h, k - 1)
 
-        @pl.when(h == halves - 1)
-        def _():
-            for r in range(1, chips):
-                cross(1, r).start()
-            for j in range(nk):
-                own_p2(j).start()
-
         @pl.loop(0, chips)
         def _(q):
             lines = [[(k, q, o) for k in range(nk)] for o in range(no)]
@@ -360,6 +358,10 @@
             pair_layer(buf, lines, 1, local(10), lambda z: gelu(z.astype(BF).astype(F32)))
             pair_layer(buf, lines, 1, local(st + 2))
             pair_layer(buf, lines, 2, local(st + 3))
+
+        @pl.when(h == 0)
+        def _():
+            forward(1)
 
         @pl.loop(0, nk + 1)
         def _(k):
@@ -378,8 +380,6 @@
                 own_a3(h, j).start()
                 for r in range(1, chips):
                     a3(h, j, r).start()
-
-    forward(1)
 
     @pl.loop(0, nk)
     def _(k):

time: 204 us -> 204 us (level)
  no operation moved by 1% of the time
where the time goes in v8:
time: 204 us; the launch traced here: 203 us
  Pallas kernels  201 us (99%)
    pallas_call x1, Pallas kernels, device_program(): pl.pallas_call(functools.partial(kernel, chips, nk), out_shape=pltpu.VMEM...  201 us

profile of v8, /device:TPU:81, one launch (start us, length us, event | category | flops | bytes accessed | tf_op | source)
XLA Modules:
  0.0 203.5 jit_solution(5675814311085816603)
XLA Ops:
  0.0 201.5 %shard_map.37 = bf16[4,16,4,32,256]{4,3,2,1,0:T(8,128)(2,1)S(1)} custom-call(bf16[4,16,4,32,256]{4,3,2,1,0:T(8,128)(2,1)} %bitcast.7, bf16[11,2,32,32,256]{4,3,2,1,0:T(8,128)(2,1)} %bitcast.5, bf16[11,2,32,32,256]{4,3,2,1,0:T(8,128)(2,1)} %bitcast.6), custom_call_target="tpu_custom_call" | custom-call | tf_op jit(solution)/shard_map/pallas_call | solution.py:437
  201.5 2.0 copy.5

commit v9 on v8

--- a/solution.py
+++ b/solution.py
@@ -98,6 +98,8 @@
     def peer(r):
         return (x + r) % chips
 
+    order = sorted(range(1, chips), key=lambda r: -min(r, chips - r))
+
     def dev(q):
         return {"sp": q * 2 + c}
 
@@ -215,7 +217,7 @@
         return pltpu.make_async_copy(t2.at[k, x], out.at[x, :, k], osem.at[2 * halves * nk + k])
 
     def send_a1(k):
-        for r in range(1, chips):
+        for r in order:
             a1(k, r).start()
 
     send_a1(0)
@@ -268,7 +270,7 @@
 
     def send_a2(h, k):
         own_a2(h, k).start()
-        for r in range(1, chips):
+        for r in order:
             a2(h, k, r).start()
 
     @pl.loop(0, nk)
@@ -378,7 +380,7 @@
                 for key in places(j):
                     put(z2.at[h], *key, own_tile(masks, get(zm.at[h], *key), get(zs2.at[h], *key), local(st + 10)(*key)).astype(BF))
                 own_a3(h, j).start()
-                for r in range(1, chips):
+                for r in order:
                     a3(h, j, r).start()
 
     @pl.loop(0, nk)
@@ -391,7 +393,7 @@
                 a3(h, k, r).wait_recv()
         t_stage(t2, 1, k, (1, 2))
         own_a4(k).start()
-        for r in range(1, chips):
+        for r in order:
             a4(k, r).start()
 
     @pl.loop(0, nk)

time: 204 us -> 204 us (level)
  no operation moved by 1% of the time
where the time goes in v9:
time: 204 us
  Pallas kernels  202 us (99%)
    pallas_call x1, Pallas kernels, device_program(): pl.pallas_call(functools.partial(kernel, chips, nk), out_shape=pltpu.VMEM...  202 us

profile of v9, /device:TPU:81, one launch (start us, length us, event | category | flops | bytes accessed | tf_op | source)
XLA Modules:
  0.0 203.9 jit_solution(5937533156844202409)
XLA Ops:
  0.0 201.9 %shard_map.37 = bf16[4,16,4,32,256]{4,3,2,1,0:T(8,128)(2,1)S(1)} custom-call(bf16[4,16,4,32,256]{4,3,2,1,0:T(8,128)(2,1)} %bitcast.7, bf16[11,2,32,32,256]{4,3,2,1,0:T(8,128)(2,1)} %bitcast.5, bf16[11,2,32,32,256]{4,3,2,1,0:T(8,128)(2,1)} %bitcast.6), custom_call_target="tpu_custom_call" | custom-call | tf_op jit(solution)/shard_map/pallas_call | solution.py:439
  201.9 2.0 copy.5
